TPU v7x, 32 devices: a whole 2x2x4 slice. The times are simulated.
32 devices in a mesh: section: 8 (over y, x, core), tp: 4 (over z).
Axes of the slice: x: 2, y: 2, z: 4, core: 2. Of those that a mesh axis runs over, the one named last changes fastest.
Arguments:
- stash: bfloat16 [8, 2, 256, 4096], P('section', None, 'tp'), may hold values from -660 to 660
- slot: int32 [8], P('section'), may hold values from 0 to 1
- doc_ids: int32 [8, 2, 256], P('section', None, 'tp'), may hold values from 0 to 3, never falling along the last dimension, each value on 1 to 128 neighbouring positions
- norm_gain: bfloat16 [4096], replicated, may hold values from 0.099609375 to 1.8984375
- w_query: bfloat16 [4096, 4096], P(None, 'tp'), may hold values from -21 to 21
- w_key: bfloat16 [4096, 1024], P(None, 'tp'), may hold values from -21 to 21
- value_weight: bfloat16 [4096, 1024], P(None, 'tp'), may hold values from -0.09375 to 0.09375
Outputs:
- received: bfloat16 [8, 256, 4096], P('section', None, 'tp')
Inputs may be any that keep to these rules, and one draw needn't show every extreme that they name: `doc_ids`: document numbers never fall along a micro-batch.
All inputs are finite; a program needn't handle non-finite values.
Results may differ from a plain program's by a relative error of at most 0.025.
The roundings to bfloat16 on the way count: a program that leaves them out, or rounds other values in their place, can miss the bound.
Values may be sent and summed in bfloat16 or wider, within the bound.
A program may use at most 64 MiB of HBM per device.

v0:
```python
import functools
import math

import jax
import jax.numpy as jnp
import numpy as np
from jax import lax
from jax.experimental import pallas as pl
from jax.experimental.pallas import tpu as pltpu
from jax.sharding import PartitionSpec as P

HEAD_SIZE = 128
ROPE_BASE = 500000.0
NORM_EPSILON = 1e-05
PIECES = 4
MESH = pl.DeviceIdType.MESH
GATHER_VMEM = 60 << 20
ATTEND_VMEM = 60 << 20
ANY = pl.BlockSpec(memory_space=pltpu.HBM)
VMEM = pl.BlockSpec(memory_space=pltpu.VMEM)


def rope_tables(length):
    half = HEAD_SIZE // 2
    freq = np.arange(half, dtype=np.float32)
    inverse = np.power(np.float32(ROPE_BASE), np.float32(-2.0) * freq / np.float32(HEAD_SIZE)).astype(np.float32)
    angles = np.arange(length, dtype=np.float32)[:, None] * inverse[None, :]
    cos, sin = np.cos(angles), np.sin(angles)
    return (
        np.concatenate([cos, cos], -1).astype(np.float32),
        np.concatenate([-sin, sin], -1).astype(np.float32),
    )


def early_pieces(sec, ns):
    pairs = ns // 2
    count = PIECES * jnp.maximum(pairs - 1 - sec // 2, 0) // pairs if pairs else 0 * sec
    return jnp.where((sec % 2 == 1) & (sec + 1 < ns), count, 0)


def kernel(
    n, ns,
    slot_ref, stash_ref, doc_hbm, gain_hbm, cos_hbm, sin_hbm, wq_ref, wk_ref, wv_ref,
    q, k, v, dcol, drow,
    raw, mine, dmine, w, xbuf, zbuf, dbuf, acc,
    raw_sem, w_sem, shift_send, right_send, left_send, recv,
    zright_send, zleft_send, zrecv,
    dshift_send, dright_send, dleft_send, drecv,
    doc_ref, gain_ref, cos_ref, sin_ref, small_sem,
):
    me = lax.axis_index("tp")
    sec = lax.axis_index("section")
    slots, rows, width = raw.shape
    pieces = PIECES
    part = width // pieces
    nq, nk = wq_ref.shape[1], wk_ref.shape[1]
    total_n = w.shape[2]
    total = n * rows
    has_right, has_left = me + 1 < n, me > 0
    has_next, has_prev = sec + 1 < ns, sec > 0
    early, early_prev = early_pieces(sec, ns), early_pieces(sec - 1, ns)

    raw_copy = pltpu.make_async_copy(stash_ref.at[0], raw, raw_sem)
    raw_copy.start()
    small = [
        pltpu.make_async_copy(src, dst, small_sem.at[i])
        for i, (src, dst) in enumerate(
            ((gain_hbm, gain_ref), (doc_hbm, doc_ref), (cos_hbm, cos_ref), (sin_hbm, sin_ref))
        )
    ]
    for c in small:
        c.start()

    bar = pltpu.get_barrier_semaphore()
    for cond, target in (
        (has_right, {"tp": me + 1}),
        (has_left, {"tp": me - 1}),
        (has_next, {"section": sec + 1}),
        (has_prev, {"section": sec - 1}),
    ):
        @pl.when(cond)
        def _():
            pl.semaphore_signal(bar, inc=1, device_id=target, device_id_type=MESH)

    def w_copies(p):
        span = pl.ds(pl.multiple_of(p * part, part), part)
        return (
            pltpu.make_async_copy(wq_ref.at[span], w.at[p, :, 0:nq], w_sem.at[p, 0]),
            pltpu.make_async_copy(wk_ref.at[span], w.at[p, :, nq:nq + nk], w_sem.at[p, 1]),
            pltpu.make_async_copy(wv_ref.at[span], w.at[p, :, nq + nk:total_n], w_sem.at[p, 2]),
        )

    @pl.when(has_prev)
    def _():
        for p in range(pieces):
            for c in w_copies(p):
                c.start()

    chosen = slot_ref[0]
    dmine[...] = jnp.zeros_like(dmine)
    for c in small:
        c.wait()
    docs = doc_ref[0, 0:1, :]
    for i in range(1, slots):
        docs = jnp.where(jnp.full(docs.shape, chosen, jnp.int32) == i, doc_ref[0, i:i + 1, :], docs)
    dmine[0:1, 0:rows] = docs
    raw_copy.wait()
    step = 16
    for r in range(0, rows, step):
        x = raw[0, r:r + step, :]
        for i in range(1, slots):
            x = jnp.where(jnp.full(x.shape, chosen, jnp.int32) == i, raw[i, r:r + step, :], x)
        x = x.astype(jnp.float32)
        scale = lax.rsqrt(jnp.mean(x * x, axis=-1, keepdims=True) + NORM_EPSILON)
        y = (x * scale * gain_ref[...].astype(jnp.float32)[None, :]).astype(jnp.bfloat16)
        for p in range(pieces):
            mine[p, r:r + step, :] = y[:, p * part:(p + 1) * part]

    def edges(a):
        return a.astype(jnp.int32)

    pl.semaphore_wait(bar, edges(has_right) + edges(has_left) + edges(has_next) + edges(has_prev))

    def remote(src, dst, ss, rs, target):
        return pltpu.make_async_remote_copy(
            src_ref=src, dst_ref=dst, send_sem=ss, recv_sem=rs, device_id=target, device_id_type=MESH
        )

    def hop(src, c, p):
        return remote(src, xbuf.at[c, p], shift_send.at[c, p], recv.at[c, p], {"section": sec + 1})

    def shift(p):
        return hop(mine.at[p], me, p)

    def zright(src, c, p):
        return remote(src, zbuf.at[c, p], zright_send.at[c, p], zrecv.at[c, p], {"tp": me + 1})

    def zleft(src, c, p):
        return remote(src, zbuf.at[c, p], zleft_send.at[c, p], zrecv.at[c, p], {"tp": me - 1})

    def dshift():
        return remote(dmine, dbuf.at[me], dshift_send, drecv.at[me], {"section": sec + 1})

    def right(c, p):
        b = xbuf.at[c, p]
        return remote(b, b, right_send.at[c, p], recv.at[c, p], {"tp": me + 1})

    def left(c, p):
        b = xbuf.at[c, p]
        return remote(b, b, left_send.at[c, p], recv.at[c, p], {"tp": me - 1})

    def dright(c):
        b = dbuf.at[c]
        return remote(b, b, dright_send.at[c], drecv.at[c], {"tp": me + 1})

    def dleft(c):
        b = dbuf.at[c]
        return remote(b, b, dleft_send.at[c], drecv.at[c], {"tp": me - 1})

    @pl.when(has_next)
    def _():
        dshift().start()
        for p in range(pieces):
            shift(p).start()
            for cond, make in ((has_right, zright), (has_left, zleft)):
                @pl.when(cond & (p < early))
                def _():
                    make(mine.at[p], me, p).start()

    tile = 256

    def compute(c, p, last):
        x = xbuf[c, p]
        for t in range(0, total_n, tile):
            acc[c, :, t:t + tile] += jnp.dot(x, w[p, :, t:t + tile], preferred_element_type=jnp.float32)

        if last is False:
            return

        @pl.when(last)
        def _():
            span = pl.ds(pl.multiple_of(c * rows, rows), rows)
            cos, sin = cos_ref[span, :], sin_ref[span, :]
            for h in range(0, nq + nk, HEAD_SIZE):
                u = acc[c, :, h:h + HEAD_SIZE]
                u = (u * cos + pltpu.roll(u, HEAD_SIZE // 2, 1) * sin).astype(jnp.bfloat16)
                if h < nq:
                    q[span, h:h + HEAD_SIZE] = u
                else:
                    k[span, h - nq:h - nq + HEAD_SIZE] = u
            v[span, :] = acc[c, :, nq + nk:total_n].astype(jnp.bfloat16)

    def own_forward():
        @pl.loop(0, pieces)
        def _(p):
            @pl.when(has_right & (p >= early_prev))
            def _():
                right(me, p).start()

            @pl.when(has_left & (p >= early_prev))
            def _():
                left(me, p).start()

    def keep_docs(c):
        drow[c] = dbuf[c]
        lanes = dbuf.shape[2]
        wide = jnp.broadcast_to(dbuf[c, 0:1, :].astype(jnp.float32), (lanes, lanes))
        dcol[pl.ds(pl.multiple_of(c * rows, rows), rows), :] = wide.T[0:rows, :]

    @pl.when(has_prev)
    def _():
        acc[...] = jnp.zeros_like(acc)
        dshift().wait_recv()

        @pl.when(has_right)
        def _():
            dright(me).start()

        @pl.when(has_left)
        def _():
            dleft(me).start()

        keep_docs(me)

        @pl.loop(0, pieces)
        def _(p):
            shift(p).wait_recv()

        own_forward()

        @pl.loop(0, pieces)
        def _(p):
            for c in w_copies(p):
                c.wait()
            compute(me, p, p == pieces - 1)

    def pass_early(d, p):
        below, above = me - d, me + d

        @pl.when(below >= 0)
        def _():
            b = zbuf.at[below, p]
            zright(b, below, p).wait_recv()

            @pl.when(has_right)
            def _():
                zright(b, below, p).start()

            hop(b, below, p).start()

        @pl.when(above < n)
        def _():
            b = zbuf.at[above, p]
            zleft(b, above, p).wait_recv()

            @pl.when(has_left)
            def _():
                zleft(b, above, p).start()

            hop(b, above, p).start()

    def take_early(below, above):
        @pl.loop(0, 2 * pieces)
        def _(i):
            c = jnp.where(i < pieces, below, above)
            p = i % pieces

            @pl.when((c >= 0) & (c < n) & (p < early_prev))
            def _():
                hop(xbuf.at[c, p], c, p).wait_recv()
                compute(c, p, False)

    @pl.when(has_prev)
    def _():
        @pl.loop(0, (n - 1) * pieces)
        def _(i):
            d, p = i // pieces + 1, i % pieces
            below, above = me - d, me + d
            late = p >= early_prev

            @pl.when(p == 0)
            def _():
                @pl.loop(0, pieces)
                def _(e):
                    @pl.when(e < early)
                    def _():
                        pass_early(d, e)

            @pl.when((below >= 0) & (p == 0))
            def _():
                dright(below).wait_recv()

                @pl.when(has_right)
                def _():
                    dright(below).start()

                keep_docs(below)

            @pl.when((above < n) & (p == 0))
            def _():
                dleft(above).wait_recv()

                @pl.when(has_left)
                def _():
                    dleft(above).start()

                keep_docs(above)

            final = p == pieces - 1

            @pl.when(final & (d == n - 1))
            def _():
                take_early(below, above)

            @pl.when(late & (below >= 0))
            def _():
                right(below, p).wait_recv()

                @pl.when(has_right)
                def _():
                    right(below, p).start()

            @pl.when(late & (above < n))
            def _():
                left(above, p).wait_recv()

                @pl.when(has_left)
                def _():
                    left(above, p).start()

            @pl.when(final & (d < n - 1))
            def _():
                take_early(below, above)

            @pl.when(late & (below >= 0))
            def _():
                compute(below, p, final)

            @pl.when(late & (above < n))
            def _():
                compute(above, p, final)

        @pl.loop(0, n * pieces)
        def _(i):
            c, p = i // pieces, i % pieces

            @pl.when(has_right & (c <= me) & (p == 0))
            def _():
                dright(c).wait_send()

            @pl.when(has_left & (c >= me) & (p == 0))
            def _():
                dleft(c).wait_send()

            @pl.when(has_right & (c <= me) & (p >= early_prev))
            def _():
                right(c, p).wait_send()

            @pl.when(has_left & (c >= me) & (p >= early_prev))
            def _():
                left(c, p).wait_send()

    @pl.when(has_next)
    def _():
        dshift().wait_send()

        @pl.loop(0, n * pieces)
        def _(i):
            c, p = i // pieces, i % pieces

            @pl.when((c == me) | (p < early))
            def _():
                hop(zbuf.at[c, p], c, p).wait_send()

            @pl.when(has_right & (c <= me) & (p < early))
            def _():
                zright(zbuf.at[c, p], c, p).wait_send()

            @pl.when(has_left & (c >= me) & (p < early))
            def _():
                zleft(zbuf.at[c, p], c, p).wait_send()


def attend(n, rows, q, k, v, dcol, drow, out_ref, s_buf, p_buf):
    sec = lax.axis_index("section")
    g = pl.program_id(0)
    total = n * rows
    group = out_ref.shape[2] // HEAD_SIZE
    block = 128 if total % 128 == 0 else total
    factor = math.log2(math.e) / math.sqrt(HEAD_SIZE)

    @pl.when(sec == 0)
    def _():
        out_ref[...] = jnp.zeros_like(out_ref)

    @pl.when(sec > 0)
    def _():
        lane_docs = jnp.concatenate([drow[c, 0:1, 0:rows] for c in range(n)], axis=1).astype(jnp.float32)
        cols = pl.ds(pl.multiple_of(g * HEAD_SIZE, HEAD_SIZE), HEAD_SIZE)
        vg = v[:, cols]
        vg = jnp.concatenate([vg, jnp.ones_like(vg)], axis=1)
        starts = range(0, total, block)
        for i in starts:
            upto = i + block
            keys = k[0:upto, cols]
            i_idx = lax.broadcasted_iota(jnp.int32, (block, upto), 0) + i
            j_idx = lax.broadcasted_iota(jnp.int32, (block, upto), 1)
            allowed = (j_idx <= i_idx) & (dcol[i:upto, 0:1] == lane_docs[:, 0:upto])
            for h in range(group):
                wide = pl.ds(pl.multiple_of((g * group + h) * HEAD_SIZE, HEAD_SIZE), HEAD_SIZE)
                raw = lax.dot_general(
                    q[i:upto, wide], keys, (((1,), (1,)), ((), ())), preferred_element_type=jnp.float32
                )
                s_buf[h, i:upto, 0:upto] = jnp.where(allowed, raw, -1e30)
        for i in starts:
            upto = i + block
            for h in range(group):
                x = s_buf[h, i:upto, 0:upto]
                e = jnp.exp2((x - jnp.max(x, axis=-1, keepdims=True)) * factor)
                p_buf[h, i:upto, 0:upto] = e.astype(jnp.bfloat16)
        for i in starts:
            upto = i + block
            for h in range(group):
                both = jnp.dot(p_buf[h, i:upto, 0:upto], vg[0:upto], preferred_element_type=jnp.float32)
                out_ref[0, i:upto, h * HEAD_SIZE:(h + 1) * HEAD_SIZE] = (
                    both[:, 0:HEAD_SIZE] / both[:, HEAD_SIZE:]
                ).astype(jnp.bfloat16)


def per_device(stash, slot, doc_ids, norm_gain, w_query, w_key, value_weight):
    n, ns = lax.axis_size("tp"), lax.axis_size("section")
    _, slots, rows, width = stash.shape
    total = n * rows
    nq, nk = w_query.shape[1], w_key.shape[1]
    total_n = nq + nk + value_weight.shape[1]
    cos, sin = rope_tables(total)
    lanes = -(-rows // 128) * 128
    bf, f32, dma = jnp.bfloat16, jnp.float32, pltpu.SemaphoreType.DMA
    part = width // PIECES
    q, k, v, dcol, drow = pl.pallas_call(
        functools.partial(kernel, n, ns),
        out_shape=(
            jax.ShapeDtypeStruct((total, nq), bf),
            jax.ShapeDtypeStruct((total, nk), bf),
            jax.ShapeDtypeStruct((total, nk), bf),
            jax.ShapeDtypeStruct((total, lanes), f32),
            jax.ShapeDtypeStruct((n, 8, lanes), jnp.int32),
        ),
        in_specs=[pl.BlockSpec(memory_space=pltpu.SMEM)] + [ANY] * 8,
        out_specs=(VMEM,) * 5,
        scratch_shapes=[
            pltpu.VMEM((slots, rows, width), bf),
            pltpu.VMEM((PIECES, rows, part), bf),
            pltpu.VMEM((8, lanes), jnp.int32),
            pltpu.VMEM((PIECES, part, total_n), bf),
            pltpu.VMEM((n, PIECES, rows, part), bf),
            pltpu.VMEM((n, PIECES, rows, part), bf),
            pltpu.VMEM((n, 8, lanes), jnp.int32),
            pltpu.VMEM((n, rows, total_n), f32),
            dma,
            dma((PIECES, 3)),
            dma((n, PIECES)),
            dma((n, PIECES)),
            dma((n, PIECES)),
            dma((n, PIECES)),
            dma((n, PIECES)),
            dma((n, PIECES)),
            dma((n, PIECES)),
            dma,
            dma((n,)),
            dma((n,)),
            dma((n,)),
            pltpu.VMEM(doc_ids.shape, jnp.int32),
            pltpu.VMEM(norm_gain.shape, bf),
            pltpu.VMEM(cos.shape, f32),
            pltpu.VMEM(sin.shape, f32),
            dma((4,)),
        ],
        compiler_params=pltpu.CompilerParams(
            collective_id=0, has_side_effects=True, vmem_limit_bytes=GATHER_VMEM
        ),
        cost_estimate=pl.CostEstimate(
            flops=2 * total * width * total_n, bytes_accessed=width * total_n * 2, transcendentals=0
        ),
    )(slot, stash, doc_ids, norm_gain, cos, sin, w_query, w_key, value_weight)
    heads = nk // HEAD_SIZE
    return pl.pallas_call(
        functools.partial(attend, n, rows),
        grid=(heads,),
        out_shape=jax.ShapeDtypeStruct((1, total, nq), bf),
        in_specs=[VMEM] * 5,
        out_specs=pl.BlockSpec((1, total, nq // heads), lambda g: (0, 0, g)),
        scratch_shapes=[
            pltpu.VMEM((nq // nk, total, total), f32),
            pltpu.VMEM((nq // nk, total, total), bf),
        ],
        compiler_params=pltpu.CompilerParams(vmem_limit_bytes=ATTEND_VMEM),
    )(q, k, v, dcol, drow)


def solution(mesh):
    placed = (
        P("section", None, "tp", None),
        P("section"),
        P("section", None, "tp"),
        P(),
        P(None, "tp"),
        P(None, "tp"),
        P(None, "tp"),
    )
    return jax.shard_map(
        per_device, mesh=mesh, in_specs=placed, out_specs=P("section", None, "tp"), check_vma=False
    )
```

profile of v0, /device:TPU:6, one launch (start us, length us, event | category | flops | bytes accessed | tf_op | source)
XLA Modules:
  0.0 43.6 jit_solution(14963425162258699473)
XLA Ops:
  0.7 39.6 %shard_map.91 = (bf16[256,1024]{1,0:T(8,128)(2,1)}, bf16[256,256]{1,0:T(8,128)(2,1)}, bf16[256,256]{1,0:T(8,128)(2,1)}, f32[256,128]{1,0:T(8,128)}, s32[4,8,128]{2,1,0:T(8,128)}) custom-call(s32[1]{0:T(128)S(6)} %copy.10.slot_ref, bf16[1,2,64,4096]{3,2,1,0:T(8,128)(2,1)} %stash_ref.1, s32[1,2,64]{2,1,0:T(2,128)} %doc_hbm.1, bf16[4096]{0:T(1024)(128)(2,1)} %gain_hbm.1, ...), custom_call_target="tpu_custom_call" | custom-call | flops 3221225472 | bytes 12582912 | tf_op jit(solution)/shard_map/pallas_call | solution.py:440
  40.2 3.3 %shard_map.92 = bf16[1,256,1024]{2,1,0:T(8,128)(2,1)} custom-call(bf16[256,1024]{1,0:T(8,128)(2,1)} %get-tuple-element.10.q, bf16[256,256]{1,0:T(8,128)(2,1)} %get-tuple-element.11.k, bf16[256,256]{1,0:T(8,128)(2,1)} %get-tuple-element.12.v, f32[256,128]{1,0:T(8,128)} %get-tuple-element.13.dcol, s32[4,8,128]{2,1,0:T(8,128)} %get-tuple-element.14.drow), custom_call_target="tpu_custom_call" | custom-call | tf_op jit(solution)/shard_map/pallas_call | solution.py:487
where the time goes:
time: 43.8 us; the launch traced here: 43.6 us
  Pallas kernels  42.9 us (98%)
  between operations  0.66 us (2%)
    pallas_call x1, Pallas kernels, per_device(): pl.pallas_call(functools.partial(kernel, n, ns), out_shape=(jax.ShapeDtyp...  39.6 us
    pallas_call x1, Pallas kernels, per_device(): pl.pallas_call(functools.partial(attend, n, rows), grid=(heads,), out_sha...  3.35 us

commit v1 on v0

--- a/solution.py
+++ b/solution.py
@@ -14,8 +14,8 @@
 NORM_EPSILON = 1e-05
 PIECES = 4
 MESH = pl.DeviceIdType.MESH
-GATHER_VMEM = 60 << 20
-ATTEND_VMEM = 60 << 20
+GATHER_VMEM = 26 << 20
+ATTEND_VMEM = 8 << 20
 ANY = pl.BlockSpec(memory_space=pltpu.HBM)
 VMEM = pl.BlockSpec(memory_space=pltpu.VMEM)
 
@@ -35,7 +35,8 @@
 def early_pieces(sec, ns):
     pairs = ns // 2
     count = PIECES * jnp.maximum(pairs - 1 - sec // 2, 0) // pairs if pairs else 0 * sec
-    return jnp.where((sec % 2 == 1) & (sec + 1 < ns), count, 0)
+    first = jnp.where((sec > 0) & (sec + 2 == ns), 1, 0)
+    return jnp.where((sec % 2 == 1) & (sec + 1 < ns), count, first)
 
 
 def kernel(
@@ -43,9 +44,9 @@
     slot_ref, stash_ref, doc_hbm, gain_hbm, cos_hbm, sin_hbm, wq_ref, wk_ref, wv_ref,
     q, k, v, dcol, drow,
     raw, mine, dmine, w, xbuf, zbuf, dbuf, acc,
-    raw_sem, w_sem, shift_send, right_send, left_send, recv,
-    zright_send, zleft_send, zrecv,
-    dshift_send, dright_send, dleft_send, drecv,
+    raw_sem, w_sem, shift_send, left_send, recv,
+    zleft_send, zrecv,
+    dshift_send, dleft_send, drecv,
     doc_ref, gain_ref, cos_ref, sin_ref, small_sem,
 ):
     me = lax.axis_index("tp")
@@ -85,16 +86,13 @@
     def w_copies(p):
         span = pl.ds(pl.multiple_of(p * part, part), part)
         return (
-            pltpu.make_async_copy(wq_ref.at[span], w.at[p, :, 0:nq], w_sem.at[p, 0]),
-            pltpu.make_async_copy(wk_ref.at[span], w.at[p, :, nq:nq + nk], w_sem.at[p, 1]),
-            pltpu.make_async_copy(wv_ref.at[span], w.at[p, :, nq + nk:total_n], w_sem.at[p, 2]),
+            pltpu.make_async_copy(wq_ref.at[span], w.at[p, :, 0:nq], w_sem.at[p]),
+            pltpu.make_async_copy(wk_ref.at[span], w.at[p, :, nq:nq + nk], w_sem.at[p]),
+            pltpu.make_async_copy(wv_ref.at[span], w.at[p, :, nq + nk:total_n], w_sem.at[p]),
         )
 
-    @pl.when(has_prev)
-    def _():
-        for p in range(pieces):
-            for c in w_copies(p):
-                c.start()
+    def w_wait(p):
+        pltpu.make_async_copy(w.at[p], w.at[p], w_sem.at[p]).wait()
 
     chosen = slot_ref[0]
     dmine[...] = jnp.zeros_like(dmine)
@@ -105,6 +103,13 @@
         docs = jnp.where(jnp.full(docs.shape, chosen, jnp.int32) == i, doc_ref[0, i:i + 1, :], docs)
     dmine[0:1, 0:rows] = docs
     raw_copy.wait()
+
+    @pl.when(has_prev)
+    def _():
+        for p in range(pieces):
+            for c in w_copies(p):
+                c.start()
+
     step = 16
     for r in range(0, rows, step):
         x = raw[0, r:r + step, :]
@@ -133,39 +138,45 @@
         return hop(mine.at[p], me, p)
 
     def zright(src, c, p):
-        return remote(src, zbuf.at[c, p], zright_send.at[c, p], zrecv.at[c, p], {"tp": me + 1})
-
-    def zleft(src, c, p):
-        return remote(src, zbuf.at[c, p], zleft_send.at[c, p], zrecv.at[c, p], {"tp": me - 1})
+        return remote(src, zbuf.at[c, p], zrecv.at[c, p], zrecv.at[c, p], {"tp": me + 1})
+
+    def zleft(src, c, p, own=False):
+        ss = zleft_send.at[p] if own else zrecv.at[c, p]
+        return remote(src, zbuf.at[c, p], ss, zrecv.at[c, p], {"tp": me - 1})
 
     def dshift():
         return remote(dmine, dbuf.at[me], dshift_send, drecv.at[me], {"section": sec + 1})
 
     def right(c, p):
         b = xbuf.at[c, p]
-        return remote(b, b, right_send.at[c, p], recv.at[c, p], {"tp": me + 1})
-
-    def left(c, p):
+        return remote(b, b, recv.at[c, p], recv.at[c, p], {"tp": me + 1})
+
+    def left(c, p, own=False):
         b = xbuf.at[c, p]
-        return remote(b, b, left_send.at[c, p], recv.at[c, p], {"tp": me - 1})
+        ss = left_send.at[p] if own else recv.at[c, p]
+        return remote(b, b, ss, recv.at[c, p], {"tp": me - 1})
 
     def dright(c):
         b = dbuf.at[c]
-        return remote(b, b, dright_send.at[c], drecv.at[c], {"tp": me + 1})
-
-    def dleft(c):
+        return remote(b, b, drecv.at[c], drecv.at[c], {"tp": me + 1})
+
+    def dleft(c, own=False):
         b = dbuf.at[c]
-        return remote(b, b, dleft_send.at[c], drecv.at[c], {"tp": me - 1})
+        return remote(b, b, dleft_send if own else drecv.at[c], drecv.at[c], {"tp": me - 1})
 
     @pl.when(has_next)
     def _():
         dshift().start()
         for p in range(pieces):
             shift(p).start()
-            for cond, make in ((has_right, zright), (has_left, zleft)):
-                @pl.when(cond & (p < early))
-                def _():
-                    make(mine.at[p], me, p).start()
+
+            @pl.when(has_right & (p < early))
+            def _():
+                zright(mine.at[p], me, p).start()
+
+            @pl.when(has_left & (p < early))
+            def _():
+                zleft(mine.at[p], me, p, True).start()
 
     tile = 256
 
@@ -190,16 +201,14 @@
                     k[span, h - nq:h - nq + HEAD_SIZE] = u
             v[span, :] = acc[c, :, nq + nk:total_n].astype(jnp.bfloat16)
 
-    def own_forward():
-        @pl.loop(0, pieces)
-        def _(p):
-            @pl.when(has_right & (p >= early_prev))
-            def _():
-                right(me, p).start()
-
-            @pl.when(has_left & (p >= early_prev))
-            def _():
-                left(me, p).start()
+    def own_forward(p):
+        @pl.when(has_right & (p >= early_prev))
+        def _():
+            right(me, p).start()
+
+        @pl.when(has_left & (p >= early_prev))
+        def _():
+            left(me, p, True).start()
 
     def keep_docs(c):
         drow[c] = dbuf[c]
@@ -218,20 +227,18 @@
 
         @pl.when(has_left)
         def _():
-            dleft(me).start()
+            dleft(me, True).start()
 
         keep_docs(me)
 
         @pl.loop(0, pieces)
         def _(p):
             shift(p).wait_recv()
-
-        own_forward()
+            own_forward(p)
 
         @pl.loop(0, pieces)
         def _(p):
-            for c in w_copies(p):
-                c.wait()
+            w_wait(p)
             compute(me, p, p == pieces - 1)
 
     def pass_early(d, p):
@@ -340,45 +347,80 @@
             def _():
                 compute(above, p, final)
 
-        @pl.loop(0, n * pieces)
-        def _(i):
-            c, p = i // pieces, i % pieces
-
-            @pl.when(has_right & (c <= me) & (p == 0))
-            def _():
-                dright(c).wait_send()
-
-            @pl.when(has_left & (c >= me) & (p == 0))
-            def _():
-                dleft(c).wait_send()
-
-            @pl.when(has_right & (c <= me) & (p >= early_prev))
-            def _():
-                right(c, p).wait_send()
-
-            @pl.when(has_left & (c >= me) & (p >= early_prev))
-            def _():
-                left(c, p).wait_send()
+        @pl.when(has_right)
+        def _():
+            dright(me).wait_send()
+
+        @pl.when(has_left)
+        def _():
+            dleft(me, True).wait_send()
+
+        for p in range(pieces):
+            @pl.when(has_right & (p >= early_prev))
+            def _():
+                right(me, p).wait_send()
+
+            @pl.when(has_left & (p >= early_prev))
+            def _():
+                left(me, p, True).wait_send()
+
+        for d in range(1, n):
+            below, above = me - d, me + d
+
+            @pl.when((below >= 0) & has_right)
+            def _():
+                dright(below).wait_send()
+                for p in range(pieces):
+                    @pl.when(p >= early_prev)
+                    def _():
+                        right(below, p).wait_send()
+
+            @pl.when((above < n) & has_left)
+            def _():
+                dleft(above).wait_send()
+                for p in range(pieces):
+                    @pl.when(p >= early_prev)
+                    def _():
+                        left(above, p).wait_send()
 
     @pl.when(has_next)
     def _():
         dshift().wait_send()
-
-        @pl.loop(0, n * pieces)
-        def _(i):
-            c, p = i // pieces, i % pieces
-
-            @pl.when((c == me) | (p < early))
-            def _():
-                hop(zbuf.at[c, p], c, p).wait_send()
-
-            @pl.when(has_right & (c <= me) & (p < early))
-            def _():
-                zright(zbuf.at[c, p], c, p).wait_send()
-
-            @pl.when(has_left & (c >= me) & (p < early))
-            def _():
-                zleft(zbuf.at[c, p], c, p).wait_send()
+        for p in range(pieces):
+            shift(p).wait_send()
+
+            @pl.when(has_right & (p < early))
+            def _():
+                zright(mine.at[p], me, p).wait_send()
+
+            @pl.when(has_left & (p < early))
+            def _():
+                zleft(mine.at[p], me, p, True).wait_send()
+
+        for d in range(1, n):
+            below, above = me - d, me + d
+
+            @pl.when((below >= 0) & (early > 0))
+            def _():
+                for p in range(pieces):
+                    @pl.when(p < early)
+                    def _():
+                        hop(zbuf.at[below, p], below, p).wait_send()
+
+                    @pl.when(has_right & (p < early))
+                    def _():
+                        zright(zbuf.at[below, p], below, p).wait_send()
+
+            @pl.when((above < n) & (early > 0))
+            def _():
+                for p in range(pieces):
+                    @pl.when(p < early)
+                    def _():
+                        hop(zbuf.at[above, p], above, p).wait_send()
+
+                    @pl.when(has_left & (p < early))
+                    def _():
+                        zleft(zbuf.at[above, p], above, p).wait_send()
 
 
 def attend(n, rows, q, k, v, dcol, drow, out_ref, s_buf, p_buf):
@@ -427,13 +469,20 @@
                 ).astype(jnp.bfloat16)
 
 
+def in_hbm(a):
+    return pltpu.with_memory_space_constraint(a, pltpu.HBM)
+
+
 def per_device(stash, slot, doc_ids, norm_gain, w_query, w_key, value_weight):
+    stash, doc_ids, norm_gain, w_query, w_key, value_weight = (
+        in_hbm(a) for a in (stash, doc_ids, norm_gain, w_query, w_key, value_weight)
+    )
     n, ns = lax.axis_size("tp"), lax.axis_size("section")
     _, slots, rows, width = stash.shape
     total = n * rows
     nq, nk = w_query.shape[1], w_key.shape[1]
     total_n = nq + nk + value_weight.shape[1]
-    cos, sin = rope_tables(total)
+    cos, sin = (in_hbm(jnp.asarray(t)) for t in rope_tables(total))
     lanes = -(-rows // 128) * 128
     bf, f32, dma = jnp.bfloat16, jnp.float32, pltpu.SemaphoreType.DMA
     part = width // PIECES
@@ -458,17 +507,14 @@
             pltpu.VMEM((n, 8, lanes), jnp.int32),
             pltpu.VMEM((n, rows, total_n), f32),
             dma,
-            dma((PIECES, 3)),
+            dma((PIECES,)),
             dma((n, PIECES)),
+            dma((PIECES,)),
             dma((n, PIECES)),
-            dma((n, PIECES)),
-            dma((n, PIECES)),
-            dma((n, PIECES)),
-            dma((n, PIECES)),
+            dma((PIECES,)),
             dma((n, PIECES)),
             dma,
-            dma((n,)),
-            dma((n,)),
+            dma,
             dma((n,)),
             pltpu.VMEM(doc_ids.shape, jnp.int32),
             pltpu.VMEM(norm_gain.shape, bf),

time: 43.8 us -> 39.3 us (0.90)
  Pallas kernels: 42.9 us -> 38.4 us
    pallas_call x1, Pallas kernels: 39.6 us -> 36.3 us  [per_device(): pl.pallas_call(functools.partial(kernel, n, ns), out_shape=(jax.ShapeDtyp...]
    pallas_call x1, Pallas kernels: 3.35 us -> 2.15 us  [per_device(): pl.pallas_call(functools.partial(attend, n, rows), grid=(heads,), out_sha...]
where the time goes in v1:
time: 39.3 us; the launch traced here: 39.1 us
  Pallas kernels  38.4 us (98%)
  between operations  0.66 us (2%)
    pallas_call x1, Pallas kernels, per_device(): pl.pallas_call(functools.partial(kernel, n, ns), out_shape=(jax.ShapeDtyp...  36.3 us
    pallas_call x1, Pallas kernels, per_device(): pl.pallas_call(functools.partial(attend, n, rows), grid=(heads,), out_sha...  2.15 us

profile of v1, /device:TPU:6, one launch (start us, length us, event | category | flops | bytes accessed | tf_op | source)
XLA Modules:
  0.0 39.1 jit_solution(5499543648930313449)
XLA Ops:
  0.7 36.3 %shard_map.91 = (bf16[256,1024]{1,0:T(8,128)(2,1)S(1)}, bf16[256,256]{1,0:T(8,128)(2,1)S(1)}, bf16[256,256]{1,0:T(8,128)(2,1)S(1)}, f32[256,128]{1,0:T(8,128)S(1)}, s32[4,8,128]{2,1,0:T(8,128)S(1)}) custom-call(s32[1]{0:T(128)S(6)} %copy.10.slot_ref, bf16[1,2,64,4096]{3,2,1,0:T(8,128)(2,1)} %stash_ref.1, s32[1,2,64]{2,1,0:T(2,128)} %doc_hbm.1, ...), custom_call_target="tpu_custom_call" | custom-call | flops 3221225472 | bytes 12582912 | tf_op jit(solution)/shard_map/pallas_call | solution.py:489
  36.9 2.2 %shard_map.92 = bf16[1,256,1024]{2,1,0:T(8,128)(2,1)} custom-call(bf16[256,1024]{1,0:T(8,128)(2,1)S(1)} %get-tuple-element.10.q, bf16[256,256]{1,0:T(8,128)(2,1)S(1)} %get-tuple-element.11.k, bf16[256,256]{1,0:T(8,128)(2,1)S(1)} %get-tuple-element.12.v, f32[256,128]{1,0:T(8,128)S(1)} %get-tuple-element.13.dcol, s32[4,8,128]{2,1,0:T(8,128)S(1)} %get-tuple-element.14.drow), custom_call_target="tpu_custom_call" | custom-call | tf_op jit(solution)/shard_map/pallas_call | solution.py:533

commit v2 on v0

v2 whole, which is shorter than its diff:
```python
import functools
import math

import jax
import jax.numpy as jnp
import numpy as np
from jax import lax
from jax.experimental import pallas as pl
from jax.experimental.pallas import tpu as pltpu
from jax.sharding import PartitionSpec as P

HEAD_SIZE = 128
ROPE_BASE = 500000.0
NORM_EPSILON = 1e-05
PIECES = 4
HELD = 1
CHUNK = 16
MESH = pl.DeviceIdType.MESH
VMEM_GRANT = 32 << 20
ANY = pl.BlockSpec(memory_space=pltpu.HBM)
VMEM = pl.BlockSpec(memory_space=pltpu.VMEM)


def rope_tables(length):
    half = HEAD_SIZE // 2
    freq = np.arange(half, dtype=np.float32)
    inverse = np.power(np.float32(ROPE_BASE), np.float32(-2.0) * freq / np.float32(HEAD_SIZE)).astype(np.float32)
    angles = np.arange(length, dtype=np.float32)[:, None] * inverse[None, :]
    cos, sin = np.cos(angles), np.sin(angles)
    return np.stack([
        np.concatenate([cos, cos], -1).astype(np.float32),
        np.concatenate([-sin, sin], -1).astype(np.float32),
    ])


def early_pieces(sec, ns):
    pairs = ns // 2
    count = PIECES * jnp.maximum(pairs - 1 - sec // 2, 0) // pairs if pairs else 0 * sec
    first = jnp.where((sec > 0) & (sec + 2 == ns), 1, 0)
    return jnp.where((sec % 2 == 1) & (sec + 1 < ns), count, first)


def kernel(
    n, ns,
    slot_ref, stash_ref, doc_hbm, gain_hbm, table_hbm, wq_ref, wk_ref, wv_ref,
    out_ref,
    raw, mine, dmine, w, xbuf, zbuf, dbuf, acc, q, k, v, dcol, drow, s_buf, p_buf,
    raw_sem, w_sem, hop_send, left_send, recv, zleft_send, zrecv,
    dshift_send, dleft_send, drecv,
    doc_ref, gain_ref, table, small_sem,
):
    me = lax.axis_index("tp")
    sec = lax.axis_index("section")
    slots, rows, width = raw.shape
    pieces = PIECES
    part = width // pieces
    nq, nk = wq_ref.shape[1], wk_ref.shape[1]
    total_n = w.shape[2]
    total = n * rows
    hold = n > 2
    even = sec % 2 == 0
    at_end = (me == 0) | (me == n - 1)
    has_right, has_left = me + 1 < n, me > 0
    has_next, has_prev = sec + 1 < ns, sec > 0
    early, early_prev = early_pieces(sec, ns), early_pieces(sec - 1, ns)

    starts = range(0, rows, CHUNK)
    raw_copies = [
        pltpu.make_async_copy(stash_ref.at[0, j, pl.ds(r, CHUNK)], raw.at[j, pl.ds(r, CHUNK)], raw_sem.at[i])
        for i, r in enumerate(starts) for j in range(slots)
    ]
    small = [
        pltpu.make_async_copy(src, dst, small_sem.at[i])
        for i, (src, dst) in enumerate(
            ((gain_hbm, gain_ref), (doc_hbm, doc_ref), (table_hbm, table))
        )
    ]
    for c in small[:1] + raw_copies + small[1:]:
        c.start()

    bar = pltpu.get_barrier_semaphore()
    for cond, target in (
        (has_right, {"tp": me + 1}),
        (has_left, {"tp": me - 1}),
        (has_next, {"section": sec + 1}),
        (has_prev, {"section": sec - 1}),
    ):
        @pl.when(cond)
        def _():
            pl.semaphore_signal(bar, inc=1, device_id=target, device_id_type=MESH)

    def w_copies():
        for p in range(pieces):
            span = pl.ds(p * part, part)
            yield pltpu.make_async_copy(wq_ref.at[span], w.at[p, :, 0:nq], w_sem)
            yield pltpu.make_async_copy(wk_ref.at[span], w.at[p, :, nq:nq + nk], w_sem)
            yield pltpu.make_async_copy(wv_ref.at[span], w.at[p, :, nq + nk:total_n], w_sem)

    for c in small[:1]:
        c.wait()
    chosen = slot_ref[0]
    for i, r in enumerate(starts):
        here = raw.at[:, pl.ds(r, CHUNK)]
        pltpu.make_async_copy(here, here, raw_sem.at[i]).wait()
        if i == len(starts) - 1:
            @pl.when(has_prev)
            def _():
                for c in w_copies():
                    c.start()
        x = raw[0, r:r + CHUNK, :]
        for j in range(1, slots):
            x = jnp.where(jnp.full(x.shape, chosen, jnp.int32) == j, raw[j, r:r + CHUNK, :], x)
        x = x.astype(jnp.float32)
        scale = lax.rsqrt(jnp.mean(x * x, axis=-1, keepdims=True) + NORM_EPSILON)
        y = (x * scale * gain_ref[...].astype(jnp.float32)[None, :]).astype(jnp.bfloat16)
        for p in range(pieces):
            mine[p, r:r + CHUNK, :] = y[:, p * part:(p + 1) * part]
    dmine[...] = jnp.zeros_like(dmine)
    for c in small[1:]:
        c.wait()
    docs = doc_ref[0, 0:1, :]
    for i in range(1, slots):
        docs = jnp.where(jnp.full(docs.shape, chosen, jnp.int32) == i, doc_ref[0, i:i + 1, :], docs)
    dmine[0:1, 0:rows] = docs

    def edges(a):
        return a.astype(jnp.int32)

    pl.semaphore_wait(bar, edges(has_right) + edges(has_left) + edges(has_next) + edges(has_prev))

    def remote(src, dst, ss, rs, target):
        return pltpu.make_async_remote_copy(
            src_ref=src, dst_ref=dst, send_sem=ss, recv_sem=rs, device_id=target, device_id_type=MESH
        )

    def sent(count, sem):
        for m in range(1, pieces + 1):
            @pl.when(count == m)
            def _():
                b = xbuf.at[0, pl.ds(0, m)]
                remote(b, b, sem, sem, {"section": sec}).wait_send()

    def hop(src, c, p):
        return remote(src, xbuf.at[c, p], hop_send.at[c], recv.at[c, p], {"section": sec + 1})

    def shift(p):
        return hop(mine.at[p], me, p)

    def zright(src, c, p):
        return remote(src, zbuf.at[c, p], zrecv.at[c, p], zrecv.at[c, p], {"tp": me + 1})

    def zleft(src, c, p, own=False):
        return remote(src, zbuf.at[c, p], zleft_send if own else zrecv.at[c, p], zrecv.at[c, p], {"tp": me - 1})

    def dshift():
        return remote(dmine, dbuf.at[me], dshift_send, drecv.at[me], {"section": sec + 1})

    def right(c, p):
        b = xbuf.at[c, p]
        return remote(b, b, recv.at[c, p], recv.at[c, p], {"tp": me + 1})

    def left(c, p, own=False):
        b = xbuf.at[c, p]
        return remote(b, b, left_send if own else recv.at[c, p], recv.at[c, p], {"tp": me - 1})

    def dright(c):
        b = dbuf.at[c]
        return remote(b, b, drecv.at[c], drecv.at[c], {"tp": me + 1})

    def dleft(c, own=False):
        b = dbuf.at[c]
        return remote(b, b, dleft_send if own else drecv.at[c], drecv.at[c], {"tp": me - 1})

    def both_ways(cond_right, cond_left, go_right, go_left):
        low = 2 * me < n

        @pl.when(cond_left & low)
        def _():
            go_left()

        @pl.when(cond_right)
        def _():
            go_right()

        @pl.when(cond_left & jnp.logical_not(low))
        def _():
            go_left()

    @pl.when(has_next)
    def _():
        dshift().start()
        for p in range(pieces - 1):
            both_ways(
                has_right & (p < early), has_left & (p < early),
                lambda: zright(mine.at[p], me, p).start(), lambda: zleft(mine.at[p], me, p, True).start(),
            )

        for p in range(pieces):
            shift(p).start()

    tile = 256

    def compute(c, p, last):
        x = xbuf[c, p]
        for t in range(0, total_n, tile):
            acc[c, :, t:t + tile] += jnp.dot(x, w[p, :, t:t + tile], preferred_element_type=jnp.float32)

        if last is False:
            return

        @pl.when(last)
        def _():
            span = pl.ds(pl.multiple_of(c * rows, rows), rows)
            cos, sin = table[0, span, :], table[1, span, :]
            for h in range(0, nq + nk, HEAD_SIZE):
                u = acc[c, :, h:h + HEAD_SIZE]
                u = (u * cos + pltpu.roll(u, HEAD_SIZE // 2, 1) * sin).astype(jnp.bfloat16)
                if h < nq:
                    q[span, h:h + HEAD_SIZE] = u
                else:
                    k[span, h - nq:h - nq + HEAD_SIZE] = u
            v[span, :] = acc[c, :, nq + nk:total_n].astype(jnp.bfloat16)

    heads = nk // HEAD_SIZE
    group = nq // nk
    factor = math.log2(math.e) / math.sqrt(HEAD_SIZE)

    def attend(i):
        span = pl.ds(pl.multiple_of(i * rows, rows), rows)
        lane_docs = jnp.concatenate([drow[c, 0:1, 0:rows] for c in range(n)], axis=1).astype(jnp.float32)
        i_idx = lax.broadcasted_iota(jnp.int32, (rows, total), 0) + i * rows
        j_idx = lax.broadcasted_iota(jnp.int32, (rows, total), 1)
        allowed = (j_idx <= i_idx) & (dcol[span, 0:1] == lane_docs)
        for g in range(heads):
            cols = slice(g * HEAD_SIZE, (g + 1) * HEAD_SIZE)
            qs = jnp.concatenate(
                [q[span, h * HEAD_SIZE:(h + 1) * HEAD_SIZE] for h in range(g * group, (g + 1) * group)], axis=0
            )
            scores = lax.dot_general(
                qs, k[:, cols], (((1,), (1,)), ((), ())), preferred_element_type=jnp.float32
            )
            for h in range(group):
                s_buf[g, h * rows:(h + 1) * rows, :] = jnp.where(
                    allowed, scores[h * rows:(h + 1) * rows], -1e30
                )
        for g in range(heads):
            for h in range(group):
                x = s_buf[g, h * rows:(h + 1) * rows, :]
                e = jnp.exp2((x - jnp.max(x, axis=-1, keepdims=True)) * factor)
                p_buf[g, h * rows:(h + 1) * rows, :] = e.astype(jnp.bfloat16)
        for g in range(heads):
            vg = v[:, g * HEAD_SIZE:(g + 1) * HEAD_SIZE]
            vg = jnp.concatenate([vg, jnp.ones_like(vg)], axis=1)
            both = jnp.dot(p_buf[g], vg, preferred_element_type=jnp.float32)
            both = (both[:, 0:HEAD_SIZE] / both[:, HEAD_SIZE:]).astype(jnp.bfloat16)
            for h in range(group):
                at = (g * group + h) * HEAD_SIZE
                out_ref[0, span, at:at + HEAD_SIZE] = both[h * rows:(h + 1) * rows]

    def attend_range(low, high):
        @pl.loop(low, high)
        def _(i):
            attend(i)

    def own_forward(p):
        held = (me == n - 2) & (p >= pieces - HELD) if hold else jnp.bool_(False)

        both_ways(
            has_right & (p >= early_prev) & jnp.logical_not(held), has_left & (p >= early_prev),
            lambda: right(me, p).start(), lambda: left(me, p, True).start(),
        )

    def weights_here():
        pltpu.make_async_copy(w, w, w_sem).wait()

    def keep_docs(c):
        drow[c] = dbuf[c]
        lanes = dbuf.shape[2]
        wide = jnp.broadcast_to(dbuf[c, 0:1, :].astype(jnp.float32), (lanes, lanes))
        dcol[pl.ds(pl.multiple_of(c * rows, rows), rows), :] = wide.T[0:rows, :]

    def pass_early(d, p):
        below, above = me - d, me + d

        @pl.when(below >= 0)
        def _():
            b = zbuf.at[below, p]
            zright(b, below, p).wait_recv()

            @pl.when(has_right)
            def _():
                zright(b, below, p).start()

            hop(b, below, p).start()

        @pl.when(above < n)
        def _():
            b = zbuf.at[above, p]
            zleft(b, above, p).wait_recv()

            @pl.when(has_left)
            def _():
                zleft(b, above, p).start()

            hop(b, above, p).start()

    def pass_all(d):
        if n > 1:
            @pl.loop(0, pieces - 1)
            def _(e):
                @pl.when(e < early)
                def _():
                    pass_early(d, e)

    @pl.when(has_prev)
    def _():
        acc[...] = jnp.zeros_like(acc)
        k[...] = jnp.zeros_like(k)
        v[...] = jnp.zeros_like(v)
        drow[...] = jnp.zeros_like(drow)

        dshift().wait_recv()

        @pl.when(has_right)
        def _():
            dright(me).start()

        @pl.when(has_left)
        def _():
            dleft(me, True).start()

        keep_docs(me)

        @pl.loop(0, pieces)
        def _(p):
            shift(p).wait_recv()
            own_forward(p)

            @pl.when(p == jnp.where(even, 0, pieces - 1))
            def _():
                pass_all(1)

        @pl.when(at_end)
        def _():
            weights_here()

            @pl.loop(0, pieces)
            def _(p):
                compute(me, p, p == pieces - 1)

        attend_range(0, jnp.where((me == 0) & (n > 1), 1, 0))

    def take_early(below, above):
        @pl.loop(0, 2 * pieces)
        def _(i):
            c = jnp.where(i < pieces, below, above)
            p = i % pieces

            @pl.when((c >= 0) & (c < n) & (p < early_prev))
            def _():
                hop(xbuf.at[c, p], c, p).wait_recv()
                compute(c, p, False)

    def drain():
        @pl.when(has_prev)
        def _():
            @pl.when(has_right)
            def _():
                dright(me).wait_send()
                for p in range(pieces):
                    @pl.when(p >= early_prev)
                    def _():
                        right(me, p).wait_send()

            @pl.when(has_left)
            def _():
                dleft(me, True).wait_send()
                sent(pieces - early_prev, left_send)

            for d in range(1, n):
                below, above = me - d, me + d

                @pl.when((below >= 0) & has_right)
                def _():
                    dright(below).wait_send()
                    for p in range(pieces):
                        @pl.when(p >= early_prev)
                        def _():
                            right(below, p).wait_send()

                @pl.when((above < n) & has_left)
                def _():
                    dleft(above).wait_send()
                    for p in range(pieces):
                        @pl.when(p >= early_prev)
                        def _():
                            left(above, p).wait_send()

        @pl.when(has_next)
        def _():
            dshift().wait_send()
            sent(pieces, hop_send.at[me])

            @pl.when(early > 0)
            def _():
                @pl.when(has_left)
                def _():
                    sent(early, zleft_send)

                @pl.when(has_right)
                def _():
                    for p in range(pieces - 1):
                        @pl.when(p < early)
                        def _():
                            zright(mine.at[p], me, p).wait_send()

                for d in range(1, n):
                    below, above = me - d, me + d

                    @pl.when(below >= 0)
                    def _():
                        sent(early, hop_send.at[below])

                        @pl.when(has_right)
                        def _():
                            for p in range(pieces - 1):
                                @pl.when(p < early)
                                def _():
                                    zright(zbuf.at[below, p], below, p).wait_send()

                    @pl.when(above < n)
                    def _():
                        sent(early, hop_send.at[above])

                        @pl.when(has_left)
                        def _():
                            for p in range(pieces - 1):
                                @pl.when(p < early)
                                def _():
                                    zleft(zbuf.at[above, p], above, p).wait_send()

    @pl.when(has_prev)
    def _():
        @pl.loop(0, (n - 1) * pieces)
        def _(i):
            d, p = i // pieces + 1, i % pieces
            below, above = me - d, me + d
            late = p >= early_prev
            final = p == pieces - 1
            from_left = late & (below >= 0)
            if hold:
                from_left = from_left & jnp.logical_not((me == n - 1) & (d == 1) & (p >= pieces - HELD))

            @pl.when(jnp.where(even, (p == pieces - 1) & (d < n - 1), (p == 0) & (d > 1)))
            def _():
                pass_all(jnp.where(even, d + 1, d))

            @pl.when((below >= 0) & (p == 0))
            def _():
                dright(below).wait_recv()

                @pl.when(has_right)
                def _():
                    dright(below).start()

                keep_docs(below)

            @pl.when((above < n) & (p == 0))
            def _():
                dleft(above).wait_recv()

                @pl.when(has_left)
                def _():
                    dleft(above).start()

                keep_docs(above)

            @pl.when((p == pieces - 2) & (d == n - 1))
            def _():
                @pl.when(at_end)
                def _():
                    drain()

                take_early(below, above)

            @pl.when(from_left)
            def _():
                right(below, p).wait_recv()

                @pl.when(has_right)
                def _():
                    right(below, p).start()

            if hold:
                @pl.when((me == n - 2) & (d == n - 2) & final)
                def _():
                    for t in range(pieces - HELD, pieces):
                        @pl.when(t >= early_prev)
                        def _():
                            right(me, t).start()

            @pl.when(late & (above < n))
            def _():
                left(above, p).wait_recv()

                @pl.when(has_left)
                def _():
                    left(above, p).start()

            @pl.when((i == 0) & jnp.logical_not(at_end))
            def _():
                weights_here()

            @pl.when(final & (d < n - 1))
            def _():
                take_early(below, above)

            @pl.when((d == min(2, n - 1)) & jnp.logical_not(at_end))
            def _():
                compute(me, p, final)

            @pl.when(from_left)
            def _():
                compute(below, p, final)

            @pl.when(late & (above < n))
            def _():
                compute(above, p, final)

            @pl.when(final & (me == 0) & (d < n - 1))
            def _():
                attend(d)

        if hold:
            @pl.when(me == n - 1)
            def _():
                attend_range(0, n - 2)

                @pl.loop(pieces - HELD, pieces)
                def _(p):
                    @pl.when(p >= early_prev)
                    def _():
                        right(n - 2, p).wait_recv()
                        compute(n - 2, p, p == pieces - 1)

        attend_range(jnp.where(me == 0, n - 1, jnp.where(me == n - 1, max(n - 2, 0), 0)), n)

    @pl.when(jnp.logical_not(has_prev & at_end))
    def _():
        drain()

    @pl.when(jnp.logical_not(has_prev))
    def _():
        out_ref[...] = jnp.zeros_like(out_ref)


def in_hbm(a):
    return pltpu.with_memory_space_constraint(a, pltpu.HBM)


def per_device(stash, slot, doc_ids, norm_gain, w_query, w_key, value_weight):
    n, ns = lax.axis_size("tp"), lax.axis_size("section")
    _, slots, rows, width = stash.shape
    total = n * rows
    nq, nk = w_query.shape[1], w_key.shape[1]
    total_n = nq + nk + value_weight.shape[1]
    table = rope_tables(total)
    lanes = -(-rows // 128) * 128
    bf, f32, dma = jnp.bfloat16, jnp.float32, pltpu.SemaphoreType.DMA
    part = width // PIECES
    heads, stacked = nk // HEAD_SIZE, nq // nk * rows
    operands = (stash, doc_ids, norm_gain, jnp.asarray(table), w_query, w_key, value_weight)
    return pl.pallas_call(
        functools.partial(kernel, n, ns),
        out_shape=jax.ShapeDtypeStruct((1, total, nq), bf),
        in_specs=[pl.BlockSpec(memory_space=pltpu.SMEM)] + [ANY] * 7,
        out_specs=VMEM,
        scratch_shapes=[
            pltpu.VMEM((slots, rows, width), bf),
            pltpu.VMEM((PIECES, rows, part), bf),
            pltpu.VMEM((8, lanes), jnp.int32),
            pltpu.VMEM((PIECES, part, total_n), bf),
            pltpu.VMEM((n, PIECES, rows, part), bf),
            pltpu.VMEM((n, PIECES - 1, rows, part), bf),
            pltpu.VMEM((n, 8, lanes), jnp.int32),
            pltpu.VMEM((n, rows, total_n), f32),
            pltpu.VMEM((total, nq), bf),
            pltpu.VMEM((total, nk), bf),
            pltpu.VMEM((total, nk), bf),
            pltpu.VMEM((total, lanes), f32),
            pltpu.VMEM((n, 8, lanes), jnp.int32),
            pltpu.VMEM((heads, stacked, total), f32),
            pltpu.VMEM((heads, stacked, total), bf),
            dma((rows // CHUNK,)),
            dma,
            dma((n,)),
            dma,
            dma((n, PIECES)),
            dma,
            dma((n, PIECES - 1)),
            dma,
            dma,
            dma((n,)),
            pltpu.VMEM(doc_ids.shape, jnp.int32),
            pltpu.VMEM(norm_gain.shape, bf),
            pltpu.VMEM(table.shape, f32),
            dma((3,)),
        ],
        compiler_params=pltpu.CompilerParams(
            collective_id=0, has_side_effects=True, vmem_limit_bytes=VMEM_GRANT
        ),
        cost_estimate=pl.CostEstimate(
            flops=2 * total * width * total_n, bytes_accessed=width * total_n * 2, transcendentals=0
        ),
    )(slot, *(in_hbm(a) for a in operands))


def solution(mesh):
    placed = (
        P("section", None, "tp", None),
        P("section"),
        P("section", None, "tp"),
        P(),
        P(None, "tp"),
        P(None, "tp"),
        P(None, "tp"),
    )
    return jax.shard_map(
        per_device, mesh=mesh, in_specs=placed, out_specs=P("section", None, "tp"), check_vma=False
    )
```

time: 43.8 us -> 38.5 us (0.88)
  Pallas kernels: 42.9 us -> 36.9 us
  local copies, waits for them, and re-layouts: 0 us -> 0.8 us
    pallas_call x2 -> x1, Pallas kernels: 42.9 us -> 36.9 us  [per_device(): pl.pallas_call(functools.partial(kernel, n, ns), out_shape=jax.ShapeDtype...]
    unnamed x0 -> x1, local copies, waits for them, and re-layouts: none -> 0.8 us
where the time goes in v2:
time: 38.5 us; the launch traced here: 38.3 us
  Pallas kernels  36.9 us (96%)
  local copies, waits for them, and re-layouts  0.8 us (2%)
  between operations  0.66 us (2%)
    pallas_call x1, Pallas kernels, per_device(): pl.pallas_call(functools.partial(kernel, n, ns), out_shape=jax.ShapeDtype...  36.9 us
    unnamed x1, local copies, waits for them, and re-layouts  0.8 us

profile of v2, /device:TPU:6, one launch (start us, length us, event | category | flops | bytes accessed | tf_op | source)
XLA Modules:
  0.0 38.3 jit_solution(959243288280204448)
XLA Ops:
  0.7 36.9 %shard_map.82 = bf16[1,256,1024]{2,1,0:T(8,128)(2,1)S(1)} custom-call(s32[1]{0:T(128)S(6)} %copy.10.slot_ref, bf16[1,2,64,4096]{3,2,1,0:T(8,128)(2,1)} %stash_ref.1, s32[1,2,64]{2,1,0:T(2,128)} %doc_hbm.1, bf16[4096]{0:T(1024)(128)(2,1)} %gain_hbm.1, f32[2,256,128]{2,1,0:T(8,128)} %constant.2.clone.table_hbm, bf16[4096,1024]{1,0:T(8,128)(2,1)} %wq_ref.1, ...), custom_call_target="tpu_custom_call" | custom-call | flops 3221225472 | bytes 12582912 | tf_op jit(solution)/shard_map/pallas_call | solution.py:573
  37.5 0.8 %copy.11 = bf16[1,256,1024]{2,1,0:T(8,128)(2,1)} copy(bf16[1,256,1024]{2,1,0:T(8,128)(2,1)S(1)} %shard_map.82) | data formatting | bytes 1048576

commit v3 on v2

--- a/solution.py
+++ b/solution.py
@@ -45,15 +45,16 @@
     slot_ref, stash_ref, doc_hbm, gain_hbm, table_hbm, wq_ref, wk_ref, wv_ref,
     out_ref,
     raw, mine, dmine, w, xbuf, zbuf, dbuf, acc, q, k, v, dcol, drow, s_buf, p_buf,
-    raw_sem, w_sem, hop_send, left_send, recv, zleft_send, zrecv,
-    dshift_send, dleft_send, drecv,
-    doc_ref, gain_ref, table, small_sem,
+    w_sem, hop_send, left_send, recv, recv2, zleft_send, zrecv,
+    dshift_send, dleft_send, drecv, table_sem,
+    doc_ref, gain_ref, table,
 ):
     me = lax.axis_index("tp")
     sec = lax.axis_index("section")
     slots, rows, width = raw.shape
     pieces = PIECES
     part = width // pieces
+    half = part // 2
     nq, nk = wq_ref.shape[1], wk_ref.shape[1]
     total_n = w.shape[2]
     total = n * rows
@@ -66,16 +67,13 @@
 
     starts = range(0, rows, CHUNK)
     raw_copies = [
-        pltpu.make_async_copy(stash_ref.at[0, j, pl.ds(r, CHUNK)], raw.at[j, pl.ds(r, CHUNK)], raw_sem.at[i])
+        pltpu.make_async_copy(stash_ref.at[0, j, pl.ds(r, CHUNK)], raw.at[j, pl.ds(r, CHUNK)], hop_send.at[i])
         for i, r in enumerate(starts) for j in range(slots)
     ]
-    small = [
-        pltpu.make_async_copy(src, dst, small_sem.at[i])
-        for i, (src, dst) in enumerate(
-            ((gain_hbm, gain_ref), (doc_hbm, doc_ref), (table_hbm, table))
-        )
-    ]
-    for c in small[:1] + raw_copies + small[1:]:
+    gain_copy = pltpu.make_async_copy(gain_hbm, gain_ref, left_send)
+    doc_copy = pltpu.make_async_copy(doc_hbm, doc_ref, zleft_send)
+    table_copy = pltpu.make_async_copy(table_hbm, table, table_sem)
+    for c in [gain_copy] + raw_copies + [doc_copy]:
         c.start()
 
     bar = pltpu.get_barrier_semaphore()
@@ -90,21 +88,21 @@
             pl.semaphore_signal(bar, inc=1, device_id=target, device_id_type=MESH)
 
     def w_copies():
-        for p in range(pieces):
-            span = pl.ds(p * part, part)
+        for p in range(2 * pieces):
+            span = pl.ds(p * half, half)
             yield pltpu.make_async_copy(wq_ref.at[span], w.at[p, :, 0:nq], w_sem)
             yield pltpu.make_async_copy(wk_ref.at[span], w.at[p, :, nq:nq + nk], w_sem)
             yield pltpu.make_async_copy(wv_ref.at[span], w.at[p, :, nq + nk:total_n], w_sem)
 
-    for c in small[:1]:
-        c.wait()
+    gain_copy.wait()
     chosen = slot_ref[0]
     for i, r in enumerate(starts):
         here = raw.at[:, pl.ds(r, CHUNK)]
-        pltpu.make_async_copy(here, here, raw_sem.at[i]).wait()
+        pltpu.make_async_copy(here, here, hop_send.at[i]).wait()
         if i == len(starts) - 1:
             @pl.when(has_prev)
             def _():
+                table_copy.start()
                 for c in w_copies():
                     c.start()
         x = raw[0, r:r + CHUNK, :]
@@ -113,11 +111,10 @@
         x = x.astype(jnp.float32)
         scale = lax.rsqrt(jnp.mean(x * x, axis=-1, keepdims=True) + NORM_EPSILON)
         y = (x * scale * gain_ref[...].astype(jnp.float32)[None, :]).astype(jnp.bfloat16)
-        for p in range(pieces):
-            mine[p, r:r + CHUNK, :] = y[:, p * part:(p + 1) * part]
+        for p in range(2 * pieces):
+            mine[p, r:r + CHUNK, :] = y[:, p * half:(p + 1) * half]
     dmine[...] = jnp.zeros_like(dmine)
-    for c in small[1:]:
-        c.wait()
+    doc_copy.wait()
     docs = doc_ref[0, 0:1, :]
     for i in range(1, slots):
         docs = jnp.where(jnp.full(docs.shape, chosen, jnp.int32) == i, doc_ref[0, i:i + 1, :], docs)
@@ -137,31 +134,82 @@
         for m in range(1, pieces + 1):
             @pl.when(count == m)
             def _():
-                b = xbuf.at[0, pl.ds(0, m)]
+                b = xbuf.at[0, pl.ds(0, 2 * m)]
                 remote(b, b, sem, sem, {"section": sec}).wait_send()
 
+    def whole(p):
+        return pl.ds(2 * p, 2)
+
+    def first():
+        return pl.ds(2 * pieces - 2, 1)
+
+    def second():
+        return pl.ds(2 * pieces - 1, 1)
+
     def hop(src, c, p):
-        return remote(src, xbuf.at[c, p], hop_send.at[c], recv.at[c, p], {"section": sec + 1})
+        return remote(src, xbuf.at[c, whole(p)], hop_send.at[c], recv.at[c, p], {"section": sec + 1})
 
     def shift(p):
-        return hop(mine.at[p], me, p)
+        return hop(mine.at[whole(p)], me, p)
+
+    def shift_last():
+        return [
+            remote(mine.at[at], xbuf.at[me, at], hop_send.at[me], rs, {"section": sec + 1})
+            for at, rs in ((first(), recv.at[me, pieces - 1]), (second(), recv2.at[me]))
+        ]
 
     def zright(src, c, p):
-        return remote(src, zbuf.at[c, p], zrecv.at[c, p], zrecv.at[c, p], {"tp": me + 1})
+        return remote(src, zbuf.at[c, whole(p)], zrecv.at[c, p], zrecv.at[c, p], {"tp": me + 1})
 
     def zleft(src, c, p, own=False):
-        return remote(src, zbuf.at[c, p], zleft_send if own else zrecv.at[c, p], zrecv.at[c, p], {"tp": me - 1})
+        return remote(
+            src, zbuf.at[c, whole(p)], zleft_send if own else zrecv.at[c, p], zrecv.at[c, p], {"tp": me - 1}
+        )
+
+    def to_right(at, c, rs):
+        b = xbuf.at[c, at]
+        return remote(b, b, rs, rs, {"tp": me + 1})
+
+    def to_left(at, c, rs, own=False):
+        b = xbuf.at[c, at]
+        return remote(b, b, left_send if own else rs, rs, {"tp": me - 1})
+
+    def right(c, p):
+        return to_right(whole(p), c, recv.at[c, p])
+
+    def left(c, p, own=False):
+        return to_left(whole(p), c, recv.at[c, p], own)
+
+    def right_last(c):
+        return [to_right(first(), c, recv.at[c, pieces - 1]), to_right(second(), c, recv2.at[c])]
+
+    def left_last(c, own=False):
+        return [to_left(first(), c, recv.at[c, pieces - 1], own), to_left(second(), c, recv2.at[c], own)]
+
+    def each(copies, act):
+        for c in copies:
+            act(c)
+
+    def pick(p, ordinary, last, act):
+        @pl.when(p < pieces - 1)
+        def _():
+            act(ordinary())
+
+        @pl.when(p == pieces - 1)
+        def _():
+            each(last(), act)
+
+    def start(c):
+        c.start()
+
+    def wait_send(c):
+        c.wait_send()
+
+    def wait_recv(c):
+        c.wait_recv()
 
     def dshift():
         return remote(dmine, dbuf.at[me], dshift_send, drecv.at[me], {"section": sec + 1})
-
-    def right(c, p):
-        b = xbuf.at[c, p]
-        return remote(b, b, recv.at[c, p], recv.at[c, p], {"tp": me + 1})
-
-    def left(c, p, own=False):
-        b = xbuf.at[c, p]
-        return remote(b, b, left_send if own else recv.at[c, p], recv.at[c, p], {"tp": me - 1})
 
     def dright(c):
         b = dbuf.at[c]
@@ -192,18 +240,23 @@
         for p in range(pieces - 1):
             both_ways(
                 has_right & (p < early), has_left & (p < early),
-                lambda: zright(mine.at[p], me, p).start(), lambda: zleft(mine.at[p], me, p, True).start(),
+                lambda: zright(mine.at[whole(p)], me, p).start(),
+                lambda: zleft(mine.at[whole(p)], me, p, True).start(),
             )
 
-        for p in range(pieces):
+        for p in range(pieces - 1):
             shift(p).start()
+        each(shift_last(), start)
 
     tile = 256
 
-    def compute(c, p, last):
-        x = xbuf[c, p]
+    def compute(c, p, last, halves=2):
+        at = pl.ds(2 * p if halves == 2 else p, halves)
+        x = xbuf[c, at]
+        x = jnp.concatenate([x[j] for j in range(halves)], axis=1)
         for t in range(0, total_n, tile):
-            acc[c, :, t:t + tile] += jnp.dot(x, w[p, :, t:t + tile], preferred_element_type=jnp.float32)
+            wt = w[at, :, t:t + tile].reshape(halves * half, tile)
+            acc[c, :, t:t + tile] += jnp.dot(x, wt, preferred_element_type=jnp.float32)
 
         if last is False:
             return
@@ -267,10 +320,12 @@
 
         both_ways(
             has_right & (p >= early_prev) & jnp.logical_not(held), has_left & (p >= early_prev),
-            lambda: right(me, p).start(), lambda: left(me, p, True).start(),
+            lambda: pick(p, lambda: right(me, p), lambda: right_last(me), start),
+            lambda: pick(p, lambda: left(me, p, True), lambda: left_last(me, True), start),
         )
 
     def weights_here():
+        table_copy.wait()
         pltpu.make_async_copy(w, w, w_sem).wait()
 
     def keep_docs(c):
@@ -284,7 +339,7 @@
 
         @pl.when(below >= 0)
         def _():
-            b = zbuf.at[below, p]
+            b = zbuf.at[below, whole(p)]
             zright(b, below, p).wait_recv()
 
             @pl.when(has_right)
@@ -295,7 +350,7 @@
 
         @pl.when(above < n)
         def _():
-            b = zbuf.at[above, p]
+            b = zbuf.at[above, whole(p)]
             zleft(b, above, p).wait_recv()
 
             @pl.when(has_left)
@@ -333,7 +388,7 @@
 
         @pl.loop(0, pieces)
         def _(p):
-            shift(p).wait_recv()
+            pick(p, lambda: shift(p), shift_last, wait_recv)
             own_forward(p)
 
             @pl.when(p == jnp.where(even, 0, pieces - 1))
@@ -350,15 +405,12 @@
 
         attend_range(0, jnp.where((me == 0) & (n > 1), 1, 0))
 
-    def take_early(below, above):
-        @pl.loop(0, 2 * pieces)
-        def _(i):
-            c = jnp.where(i < pieces, below, above)
-            p = i % pieces
-
-            @pl.when((c >= 0) & (c < n) & (p < early_prev))
-            def _():
-                hop(xbuf.at[c, p], c, p).wait_recv()
+    def take_early(c):
+        @pl.loop(0, pieces - 1)
+        def _(p):
+            @pl.when(p < early_prev)
+            def _():
+                hop(xbuf.at[c, whole(p)], c, p).wait_recv()
                 compute(c, p, False)
 
     def drain():
@@ -367,10 +419,11 @@
             @pl.when(has_right)
             def _():
                 dright(me).wait_send()
-                for p in range(pieces):
+                for p in range(pieces - 1):
                     @pl.when(p >= early_prev)
                     def _():
                         right(me, p).wait_send()
+                each(right_last(me), wait_send)
 
             @pl.when(has_left)
             def _():
@@ -383,18 +436,20 @@
                 @pl.when((below >= 0) & has_right)
                 def _():
                     dright(below).wait_send()
-                    for p in range(pieces):
+                    for p in range(pieces - 1):
                         @pl.when(p >= early_prev)
                         def _():
                             right(below, p).wait_send()
+                    each(right_last(below), wait_send)
 
                 @pl.when((above < n) & has_left)
                 def _():
                     dleft(above).wait_send()
-                    for p in range(pieces):
+                    for p in range(pieces - 1):
                         @pl.when(p >= early_prev)
                         def _():
                             left(above, p).wait_send()
+                    each(left_last(above), wait_send)
 
         @pl.when(has_next)
         def _():
@@ -412,7 +467,7 @@
                     for p in range(pieces - 1):
                         @pl.when(p < early)
                         def _():
-                            zright(mine.at[p], me, p).wait_send()
+                            zright(mine.at[whole(p)], me, p).wait_send()
 
                 for d in range(1, n):
                     below, above = me - d, me + d
@@ -426,7 +481,7 @@
                             for p in range(pieces - 1):
                                 @pl.when(p < early)
                                 def _():
-                                    zright(zbuf.at[below, p], below, p).wait_send()
+                                    zright(zbuf.at[below, whole(p)], below, p).wait_send()
 
                     @pl.when(above < n)
                     def _():
@@ -437,9 +492,76 @@
                             for p in range(pieces - 1):
                                 @pl.when(p < early)
                                 def _():
-                                    zleft(zbuf.at[above, p], above, p).wait_send()
-
-    @pl.when(has_prev)
+                                    zleft(zbuf.at[above, whole(p)], above, p).wait_send()
+
+    def take_last(c):
+        for t, r in enumerate(right_last(c)):
+            r.wait_recv()
+            compute(c, 2 * pieces - 2 + t, jnp.bool_(t == 1), 1)
+
+    def pass_now(d, p):
+        @pl.when(jnp.where(even, (p == pieces - 1) & (d < n - 1), (p == 0) & (d > 1)))
+        def _():
+            pass_all(jnp.where(even, d + 1, d))
+
+    @pl.when(has_prev & at_end)
+    def _():
+        drain_at = jnp.where(even & (n > 2), (n - 3) * pieces + pieces - 1, (n - 2) * pieces + 1)
+        ahead = (early_prev == 1) & (n > 2)
+
+        @pl.loop(0, (n - 1) * pieces)
+        def _(i):
+            d, p = i // pieces + 1, i % pieces
+            c = jnp.where(me == 0, d, n - 1 - d)
+            go = p >= early_prev
+            if hold:
+                go = go & jnp.logical_not((me == n - 1) & (d == 1) & (p >= pieces - HELD))
+
+            pass_now(d, p)
+
+            @pl.when(p == 0)
+            def _():
+                dright(c).wait_recv()
+                keep_docs(c)
+
+            @pl.when(i == drain_at)
+            def _():
+                drain()
+
+            sooner = ahead & (d == n - 2) & (p == pieces - 1)
+            usual = (p == pieces - 2) & jnp.logical_not(ahead & (d == n - 1))
+
+            @pl.when((early_prev > 0) & (sooner | usual))
+            def _():
+                take_early(jnp.where(sooner, jnp.where(me == 0, n - 1, 0), c))
+
+            @pl.when(go & (p < pieces - 1))
+            def _():
+                right(c, p).wait_recv()
+                compute(c, p, False)
+
+            @pl.when(go & (p == pieces - 1))
+            def _():
+                take_last(c)
+
+            @pl.when((p == pieces - 1) & (me == 0) & (d < n - 1))
+            def _():
+                attend(d)
+
+        if hold:
+            @pl.when(me == n - 1)
+            def _():
+                attend_range(0, n - 2)
+
+                for p in range(pieces - HELD, pieces - 1):
+                    @pl.when(p >= early_prev)
+                    def _():
+                        right(n - 2, p).wait_recv()
+                        compute(n - 2, p, False)
+
+                take_last(n - 2)
+
+    @pl.when(has_prev & jnp.logical_not(at_end))
     def _():
         @pl.loop(0, (n - 1) * pieces)
         def _(i):
@@ -447,79 +569,61 @@
             below, above = me - d, me + d
             late = p >= early_prev
             final = p == pieces - 1
-            from_left = late & (below >= 0)
-            if hold:
-                from_left = from_left & jnp.logical_not((me == n - 1) & (d == 1) & (p >= pieces - HELD))
-
-            @pl.when(jnp.where(even, (p == pieces - 1) & (d < n - 1), (p == 0) & (d > 1)))
-            def _():
-                pass_all(jnp.where(even, d + 1, d))
+
+            pass_now(d, p)
 
             @pl.when((below >= 0) & (p == 0))
             def _():
                 dright(below).wait_recv()
-
-                @pl.when(has_right)
-                def _():
-                    dright(below).start()
-
+                dright(below).start()
                 keep_docs(below)
 
             @pl.when((above < n) & (p == 0))
             def _():
                 dleft(above).wait_recv()
-
-                @pl.when(has_left)
-                def _():
-                    dleft(above).start()
-
+                dleft(above).start()
                 keep_docs(above)
 
-            @pl.when((p == pieces - 2) & (d == n - 1))
-            def _():
-                @pl.when(at_end)
-                def _():
-                    drain()
-
-                take_early(below, above)
-
-            @pl.when(from_left)
-            def _():
-                right(below, p).wait_recv()
-
-                @pl.when(has_right)
-                def _():
-                    right(below, p).start()
+            def forward(c):
+                c.wait_recv()
+                c.start()
+
+            @pl.when(late & (below >= 0))
+            def _():
+                pick(p, lambda: right(below, p), lambda: right_last(below), forward)
 
             if hold:
                 @pl.when((me == n - 2) & (d == n - 2) & final)
                 def _():
-                    for t in range(pieces - HELD, pieces):
+                    for t in range(pieces - HELD, pieces - 1):
                         @pl.when(t >= early_prev)
                         def _():
                             right(me, t).start()
+                    each(right_last(me), start)
 
             @pl.when(late & (above < n))
             def _():
-                left(above, p).wait_recv()
-
-                @pl.when(has_left)
+                pick(p, lambda: left(above, p), lambda: left_last(above), forward)
+
+            @pl.when(i == 0)
+            def _():
+                weights_here()
+
+            @pl.when((p == pieces - 2) & (early_prev > 0))
+            def _():
+                @pl.when(below >= 0)
                 def _():
-                    left(above, p).start()
-
-            @pl.when((i == 0) & jnp.logical_not(at_end))
-            def _():
-                weights_here()
-
-            @pl.when(final & (d < n - 1))
-            def _():
-                take_early(below, above)
-
-            @pl.when((d == min(2, n - 1)) & jnp.logical_not(at_end))
+                    take_early(below)
+
+                @pl.when(above < n)
+                def _():
+                    take_early(above)
+
+            @pl.when(d == min(2, n - 1))
             def _():
                 compute(me, p, final)
 
-            @pl.when(from_left)
+            @pl.when(late & (below >= 0))
             def _():
                 compute(below, p, final)
 
@@ -527,22 +631,8 @@
             def _():
                 compute(above, p, final)
 
-            @pl.when(final & (me == 0) & (d < n - 1))
-            def _():
-                attend(d)
-
-        if hold:
-            @pl.when(me == n - 1)
-            def _():
-                attend_range(0, n - 2)
-
-                @pl.loop(pieces - HELD, pieces)
-                def _(p):
-                    @pl.when(p >= early_prev)
-                    def _():
-                        right(n - 2, p).wait_recv()
-                        compute(n - 2, p, p == pieces - 1)
-
+    @pl.when(has_prev)
+    def _():
         attend_range(jnp.where(me == 0, n - 1, jnp.where(me == n - 1, max(n - 2, 0), 0)), n)
 
     @pl.when(jnp.logical_not(has_prev & at_end))
@@ -577,11 +667,11 @@
         out_specs=VMEM,
         scratch_shapes=[
             pltpu.VMEM((slots, rows, width), bf),
-            pltpu.VMEM((PIECES, rows, part), bf),
+            pltpu.VMEM((2 * PIECES, rows, part // 2), bf),
             pltpu.VMEM((8, lanes), jnp.int32),
-            pltpu.VMEM((PIECES, part, total_n), bf),
-            pltpu.VMEM((n, PIECES, rows, part), bf),
-            pltpu.VMEM((n, PIECES - 1, rows, part), bf),
+            pltpu.VMEM((2 * PIECES, part // 2, total_n), bf),
+            pltpu.VMEM((n, 2 * PIECES, rows, part // 2), bf),
+            pltpu.VMEM((n, 2 * PIECES - 2, rows, part // 2), bf),
             pltpu.VMEM((n, 8, lanes), jnp.int32),
             pltpu.VMEM((n, rows, total_n), f32),
             pltpu.VMEM((total, nq), bf),
@@ -591,20 +681,20 @@
             pltpu.VMEM((n, 8, lanes), jnp.int32),
             pltpu.VMEM((heads, stacked, total), f32),
             pltpu.VMEM((heads, stacked, total), bf),
-            dma((rows // CHUNK,)),
             dma,
-            dma((n,)),
+            dma((max(n, rows // CHUNK),)),
             dma,
             dma((n, PIECES)),
+            dma((n,)),
             dma,
             dma((n, PIECES - 1)),
             dma,
             dma,
             dma((n,)),
+            dma,
             pltpu.VMEM(doc_ids.shape, jnp.int32),
             pltpu.VMEM(norm_gain.shape, bf),
             pltpu.VMEM(table.shape, f32),
-            dma((3,)),
         ],
         compiler_params=pltpu.CompilerParams(
             collective_id=0, has_side_effects=True, vmem_limit_bytes=VMEM_GRANT

time: 38.5 us -> 37.6 us (0.977)
  Pallas kernels: 36.9 us -> 35.9 us
    pallas_call x1, Pallas kernels: 36.9 us -> 35.9 us  [per_device(): pl.pallas_call(functools.partial(kernel, n, ns), out_shape=jax.ShapeDtype...]
where the time goes in v3:
time: 37.6 us; the launch traced here: 37.4 us
  Pallas kernels  35.9 us (95%)
  local copies, waits for them, and re-layouts  0.8 us (2%)
  between operations  0.66 us (2%)
    pallas_call x1, Pallas kernels, per_device(): pl.pallas_call(functools.partial(kernel, n, ns), out_shape=jax.ShapeDtype...  35.9 us
    unnamed x1, local copies, waits for them, and re-layouts  0.8 us

profile of v3, /device:TPU:6, one launch (start us, length us, event | category | flops | bytes accessed | tf_op | source)
XLA Modules:
  0.0 37.4 jit_solution(11824467904026419023)
XLA Ops:
  0.7 35.9 %shard_map.82 = bf16[1,256,1024]{2,1,0:T(8,128)(2,1)S(1)} custom-call(s32[1]{0:T(128)S(6)} %copy.10.slot_ref, bf16[1,2,64,4096]{3,2,1,0:T(8,128)(2,1)} %stash_ref.1, s32[1,2,64]{2,1,0:T(2,128)} %doc_hbm.1, bf16[4096]{0:T(1024)(128)(2,1)} %gain_hbm.1, f32[2,256,128]{2,1,0:T(8,128)} %constant.2.clone.table_hbm, bf16[4096,1024]{1,0:T(8,128)(2,1)} %wq_ref.1, ...), custom_call_target="tpu_custom_call" | custom-call | flops 3221225472 | bytes 12582912 | tf_op jit(solution)/shard_map/pallas_call | solution.py:663
  36.6 0.8 %copy.11 = bf16[1,256,1024]{2,1,0:T(8,128)(2,1)} copy(bf16[1,256,1024]{2,1,0:T(8,128)(2,1)S(1)} %shard_map.82) | data formatting | bytes 1048576

commit v4 on v3

--- a/solution.py
+++ b/solution.py
@@ -46,7 +46,7 @@
     out_ref,
     raw, mine, dmine, w, xbuf, zbuf, dbuf, acc, q, k, v, dcol, drow, s_buf, p_buf,
     w_sem, hop_send, left_send, recv, recv2, zleft_send, zrecv,
-    dshift_send, dleft_send, drecv, table_sem,
+    dshift_send, dleft_send, drecv, table_sem, ready,
     doc_ref, gain_ref, table,
 ):
     me = lax.axis_index("tp")
@@ -59,33 +59,31 @@
     total_n = w.shape[2]
     total = n * rows
     hold = n > 2
-    even = sec % 2 == 0
+    even, odd = sec % 2 == 0, sec % 2 == 1
     at_end = (me == 0) | (me == n - 1)
     has_right, has_left = me + 1 < n, me > 0
     has_next, has_prev = sec + 1 < ns, sec > 0
     early, early_prev = early_pieces(sec, ns), early_pieces(sec - 1, ns)
-
-    starts = range(0, rows, CHUNK)
-    raw_copies = [
-        pltpu.make_async_copy(stash_ref.at[0, j, pl.ds(r, CHUNK)], raw.at[j, pl.ds(r, CHUNK)], hop_send.at[i])
-        for i, r in enumerate(starts) for j in range(slots)
-    ]
-    gain_copy = pltpu.make_async_copy(gain_hbm, gain_ref, left_send)
-    doc_copy = pltpu.make_async_copy(doc_hbm, doc_ref, zleft_send)
-    table_copy = pltpu.make_async_copy(table_hbm, table, table_sem)
-    for c in [gain_copy] + raw_copies + [doc_copy]:
-        c.start()
+    greet, greet_prev = odd & (early >= 2), even & (early_prev >= 2)
 
     bar = pltpu.get_barrier_semaphore()
     for cond, target in (
         (has_right, {"tp": me + 1}),
         (has_left, {"tp": me - 1}),
-        (has_next, {"section": sec + 1}),
-        (has_prev, {"section": sec - 1}),
+        (has_next & greet, {"section": sec + 1}),
+        (has_prev & jnp.logical_not(greet_prev), {"section": sec - 1}),
     ):
         @pl.when(cond)
         def _():
             pl.semaphore_signal(bar, inc=1, device_id=target, device_id_type=MESH)
+
+    starts = range(0, rows, CHUNK)
+    raw_copies = [pltpu.make_async_copy(stash_ref.at[0, :, pl.ds(r, CHUNK)], raw.at[:, pl.ds(r, CHUNK)], hop_send.at[0]) for r in starts]
+    gain_copy = pltpu.make_async_copy(gain_hbm, gain_ref, left_send)
+    doc_copy = pltpu.make_async_copy(doc_hbm, doc_ref, zleft_send)
+    table_copy = pltpu.make_async_copy(table_hbm, table, table_sem)
+    for c in raw_copies + [gain_copy, doc_copy]:
+        c.start()
 
     def w_copies():
         for p in range(2 * pieces):
@@ -96,10 +94,9 @@
 
     gain_copy.wait()
     chosen = slot_ref[0]
+    pltpu.make_async_copy(raw, raw, hop_send.at[0]).wait()
     for i, r in enumerate(starts):
-        here = raw.at[:, pl.ds(r, CHUNK)]
-        pltpu.make_async_copy(here, here, hop_send.at[i]).wait()
-        if i == len(starts) - 1:
+        if i == 0:
             @pl.when(has_prev)
             def _():
                 table_copy.start()
@@ -123,7 +120,14 @@
     def edges(a):
         return a.astype(jnp.int32)
 
-    pl.semaphore_wait(bar, edges(has_right) + edges(has_left) + edges(has_next) + edges(has_prev))
+    pl.semaphore_wait(
+        bar,
+        edges(has_right) + edges(has_left) + edges(has_next & jnp.logical_not(greet)) + edges(has_prev & greet_prev),
+    )
+
+    @pl.when(has_prev & greet_prev)
+    def _():
+        pl.semaphore_signal(ready, inc=1, device_id={"section": sec - 1}, device_id_type=MESH)
 
     def remote(src, dst, ss, rs, target):
         return pltpu.make_async_remote_copy(
@@ -236,17 +240,40 @@
 
     @pl.when(has_next)
     def _():
-        dshift().start()
-        for p in range(pieces - 1):
-            both_ways(
-                has_right & (p < early), has_left & (p < early),
-                lambda: zright(mine.at[whole(p)], me, p).start(),
-                lambda: zleft(mine.at[whole(p)], me, p, True).start(),
-            )
-
-        for p in range(pieces - 1):
-            shift(p).start()
-        each(shift_last(), start)
+        def own_ways():
+            for p in range(pieces - 1):
+                both_ways(
+                    has_right & (p < early), has_left & (p < early),
+                    lambda: zright(mine.at[whole(p)], me, p).start(),
+                    lambda: zleft(mine.at[whole(p)], me, p, True).start(),
+                )
+
+        def hops():
+            @pl.when(greet)
+            def _():
+                pl.semaphore_wait(ready, 1)
+
+            dshift().start()
+            for p in range(pieces - 1):
+                @pl.when(p >= early)
+                def _():
+                    shift(p).start()
+
+            each(shift_last(), start)
+            for p in range(pieces - 1):
+                @pl.when(p < early)
+                def _():
+                    shift(p).start()
+
+        @pl.when(odd)
+        def _():
+            own_ways()
+            hops()
+
+        @pl.when(even)
+        def _():
+            hops()
+            own_ways()
 
     tile = 256
 
@@ -261,8 +288,7 @@
         if last is False:
             return
 
-        @pl.when(last)
-        def _():
+        def finish():
             span = pl.ds(pl.multiple_of(c * rows, rows), rows)
             cos, sin = table[0, span, :], table[1, span, :]
             for h in range(0, nq + nk, HEAD_SIZE):
@@ -273,6 +299,11 @@
                 else:
                     k[span, h - nq:h - nq + HEAD_SIZE] = u
             v[span, :] = acc[c, :, nq + nk:total_n].astype(jnp.bfloat16)
+
+        if last is True:
+            finish()
+        else:
+            pl.when(last)(finish)
 
     heads = nk // HEAD_SIZE
     group = nq // nk
@@ -319,10 +350,17 @@
         held = (me == n - 2) & (p >= pieces - HELD) if hold else jnp.bool_(False)
 
         both_ways(
-            has_right & (p >= early_prev) & jnp.logical_not(held), has_left & (p >= early_prev),
+            has_right & jnp.logical_not(held), has_left,
             lambda: pick(p, lambda: right(me, p), lambda: right_last(me), start),
             lambda: pick(p, lambda: left(me, p, True), lambda: left_last(me, True), start),
         )
+
+    def compute_own(p):
+        @pl.when(p < early_prev)
+        def _():
+            shift(p).wait_recv()
+
+        compute(me, p, p == pieces - 1)
 
     def weights_here():
         table_copy.wait()
@@ -386,12 +424,12 @@
 
         keep_docs(me)
 
-        @pl.loop(0, pieces)
+        @pl.loop(early_prev, pieces)
         def _(p):
             pick(p, lambda: shift(p), shift_last, wait_recv)
             own_forward(p)
 
-            @pl.when(p == jnp.where(even, 0, pieces - 1))
+            @pl.when(p == jnp.where(even, early_prev, pieces - 1))
             def _():
                 pass_all(1)
 
@@ -401,7 +439,7 @@
 
             @pl.loop(0, pieces)
             def _(p):
-                compute(me, p, p == pieces - 1)
+                compute_own(p)
 
         attend_range(0, jnp.where((me == 0) & (n > 1), 1, 0))
 
@@ -497,7 +535,7 @@
     def take_last(c):
         for t, r in enumerate(right_last(c)):
             r.wait_recv()
-            compute(c, 2 * pieces - 2 + t, jnp.bool_(t == 1), 1)
+            compute(c, 2 * pieces - 2 + t, t == 1, 1)
 
     def pass_now(d, p):
         @pl.when(jnp.where(even, (p == pieces - 1) & (d < n - 1), (p == 0) & (d > 1)))
@@ -540,7 +578,7 @@
                 right(c, p).wait_recv()
                 compute(c, p, False)
 
-            @pl.when(go & (p == pieces - 1))
+            @pl.when(go & (p == pieces - 1) & (i < (n - 1) * pieces - 1))
             def _():
                 take_last(c)
 
@@ -548,11 +586,16 @@
             def _():
                 attend(d)
 
-        if hold:
-            @pl.when(me == n - 1)
-            def _():
+        @pl.when(me == 0)
+        def _():
+            take_last(n - 1)
+            attend(n - 1)
+
+        @pl.when(me > 0)
+        def _():
+            take_last(0)
+            if hold:
                 attend_range(0, n - 2)
-
                 for p in range(pieces - HELD, pieces - 1):
                     @pl.when(p >= early_prev)
                     def _():
@@ -560,6 +603,8 @@
                         compute(n - 2, p, False)
 
                 take_last(n - 2)
+            for t in range(max(n - 2, 0), n):
+                attend(t)
 
     @pl.when(has_prev & jnp.logical_not(at_end))
     def _():
@@ -621,7 +666,7 @@
 
             @pl.when(d == min(2, n - 1))
             def _():
-                compute(me, p, final)
+                compute_own(p)
 
             @pl.when(late & (below >= 0))
             def _():
@@ -631,9 +676,7 @@
             def _():
                 compute(above, p, final)
 
-    @pl.when(has_prev)
-    def _():
-        attend_range(jnp.where(me == 0, n - 1, jnp.where(me == n - 1, max(n - 2, 0), 0)), n)
+        attend_range(0, n)
 
     @pl.when(jnp.logical_not(has_prev & at_end))
     def _():
@@ -692,6 +735,7 @@
             dma,
             dma((n,)),
             dma,
+            pltpu.SemaphoreType.REGULAR,
             pltpu.VMEM(doc_ids.shape, jnp.int32),
             pltpu.VMEM(norm_gain.shape, bf),
             pltpu.VMEM(table.shape, f32),

time: 37.6 us -> 37.5 us (level)
  no operation moved by 1% of the time
where the time goes in v4:
time: 37.5 us; the launch traced here: 37.3 us
  Pallas kernels  35.9 us (96%)
  local copies, waits for them, and re-layouts  0.8 us (2%)
  between operations  0.66 us (2%)
    pallas_call x1, Pallas kernels, per_device(): pl.pallas_call(functools.partial(kernel, n, ns), out_shape=jax.ShapeDtype...  35.9 us
    unnamed x1, local copies, waits for them, and re-layouts  0.8 us

profile of v4, /device:TPU:6, one launch (start us, length us, event | category | flops | bytes accessed | tf_op | source)
XLA Modules:
  0.0 37.3 jit_solution(14999007246731313635)
XLA Ops:
  0.7 35.9 %shard_map.82 = bf16[1,256,1024]{2,1,0:T(8,128)(2,1)S(1)} custom-call(s32[1]{0:T(128)S(6)} %copy.10.slot_ref, bf16[1,2,64,4096]{3,2,1,0:T(8,128)(2,1)} %stash_ref.1, s32[1,2,64]{2,1,0:T(2,128)} %doc_hbm.1, bf16[4096]{0:T(1024)(128)(2,1)} %gain_hbm.1, f32[2,256,128]{2,1,0:T(8,128)} %constant.2.clone.table_hbm, bf16[4096,1024]{1,0:T(8,128)(2,1)} %wq_ref.1, ...), custom_call_target="tpu_custom_call" | custom-call | flops 3221225472 | bytes 12582912 | tf_op jit(solution)/shard_map/pallas_call | solution.py:706
  36.5 0.8 %copy.11 = bf16[1,256,1024]{2,1,0:T(8,128)(2,1)} copy(bf16[1,256,1024]{2,1,0:T(8,128)(2,1)S(1)} %shard_map.82) | data formatting | bytes 1048576

commit v5 on v4

--- a/solution.py
+++ b/solution.py
@@ -542,6 +542,86 @@
         def _():
             pass_all(jnp.where(even, d + 1, d))
 
+    @pl.when(has_prev & jnp.logical_not(at_end))
+    def _():
+        @pl.loop(0, (n - 1) * pieces)
+        def _(i):
+            d, p = i // pieces + 1, i % pieces
+            below, above = me - d, me + d
+            late = p >= early_prev
+            final = p == pieces - 1
+
+            pass_now(d, p)
+
+            @pl.when((below >= 0) & (p == 0))
+            def _():
+                dright(below).wait_recv()
+                dright(below).start()
+                keep_docs(below)
+
+            @pl.when((above < n) & (p == 0))
+            def _():
+                dleft(above).wait_recv()
+                dleft(above).start()
+                keep_docs(above)
+
+            def forward(c):
+                c.wait_recv()
+                c.start()
+
+            @pl.when(late & (below >= 0))
+            def _():
+                pick(p, lambda: right(below, p), lambda: right_last(below), forward)
+
+            if hold:
+                @pl.when((me == n - 2) & (d == n - 2) & final)
+                def _():
+                    for t in range(pieces - HELD, pieces - 1):
+                        @pl.when(t >= early_prev)
+                        def _():
+                            right(me, t).start()
+                    each(right_last(me), start)
+
+            @pl.when(late & (above < n))
+            def _():
+                pick(p, lambda: left(above, p), lambda: left_last(above), forward)
+
+            @pl.when(i == 0)
+            def _():
+                weights_here()
+
+            @pl.when((p == pieces - 2) & (early_prev > 0))
+            def _():
+                @pl.when(below >= 0)
+                def _():
+                    take_early(below)
+
+                @pl.when(above < n)
+                def _():
+                    take_early(above)
+
+            @pl.when(d == min(2, n - 1))
+            def _():
+                compute_own(p)
+
+            @pl.when(late & (below >= 0))
+            def _():
+                compute(below, p, final)
+
+            @pl.when(late & (above < n))
+            def _():
+                compute(above, p, final)
+
+        attend_range(0, n)
+
+    @pl.when(jnp.logical_not(has_prev & at_end))
+    def _():
+        drain()
+
+    @pl.when(jnp.logical_not(has_prev))
+    def _():
+        out_ref[...] = jnp.zeros_like(out_ref)
+
     @pl.when(has_prev & at_end)
     def _():
         drain_at = jnp.where(even & (n > 2), (n - 3) * pieces + pieces - 1, (n - 2) * pieces + 1)
@@ -585,11 +665,6 @@
             @pl.when((p == pieces - 1) & (me == 0) & (d < n - 1))
             def _():
                 attend(d)
-
-        @pl.when(me == 0)
-        def _():
-            take_last(n - 1)
-            attend(n - 1)
 
         @pl.when(me > 0)
         def _():
@@ -606,85 +681,10 @@
             for t in range(max(n - 2, 0), n):
                 attend(t)
 
-    @pl.when(has_prev & jnp.logical_not(at_end))
-    def _():
-        @pl.loop(0, (n - 1) * pieces)
-        def _(i):
-            d, p = i // pieces + 1, i % pieces
-            below, above = me - d, me + d
-            late = p >= early_prev
-            final = p == pieces - 1
-
-            pass_now(d, p)
-
-            @pl.when((below >= 0) & (p == 0))
-            def _():
-                dright(below).wait_recv()
-                dright(below).start()
-                keep_docs(below)
-
-            @pl.when((above < n) & (p == 0))
-            def _():
-                dleft(above).wait_recv()
-                dleft(above).start()
-                keep_docs(above)
-
-            def forward(c):
-                c.wait_recv()
-                c.start()
-
-            @pl.when(late & (below >= 0))
-            def _():
-                pick(p, lambda: right(below, p), lambda: right_last(below), forward)
-
-            if hold:
-                @pl.when((me == n - 2) & (d == n - 2) & final)
-                def _():
-                    for t in range(pieces - HELD, pieces - 1):
-                        @pl.when(t >= early_prev)
-                        def _():
-                            right(me, t).start()
-                    each(right_last(me), start)
-
-            @pl.when(late & (above < n))
-            def _():
-                pick(p, lambda: left(above, p), lambda: left_last(above), forward)
-
-            @pl.when(i == 0)
-            def _():
-                weights_here()
-
-            @pl.when((p == pieces - 2) & (early_prev > 0))
-            def _():
-                @pl.when(below >= 0)
-                def _():
-                    take_early(below)
-
-                @pl.when(above < n)
-                def _():
-                    take_early(above)
-
-            @pl.when(d == min(2, n - 1))
-            def _():
-                compute_own(p)
-
-            @pl.when(late & (below >= 0))
-            def _():
-                compute(below, p, final)
-
-            @pl.when(late & (above < n))
-            def _():
-                compute(above, p, final)
-
-        attend_range(0, n)
-
-    @pl.when(jnp.logical_not(has_prev & at_end))
-    def _():
-        drain()
-
-    @pl.when(jnp.logical_not(has_prev))
-    def _():
-        out_ref[...] = jnp.zeros_like(out_ref)
+        @pl.when(me == 0)
+        def _():
+            take_last(n - 1)
+            attend(n - 1)
 
 
 def in_hbm(a):

time: 37.5 us -> 37.5 us (level)
  no operation moved by 1% of the time
where the time goes in v5:
time: 37.5 us; the launch traced here: 37.3 us
  Pallas kernels  35.8 us (95%)
  local copies, waits for them, and re-layouts  0.8 us (2%)
  between operations  0.66 us (2%)
    pallas_call x1, Pallas kernels, per_device(): pl.pallas_call(functools.partial(kernel, n, ns), out_shape=jax.ShapeDtype...  35.8 us
    unnamed x1, local copies, waits for them, and re-layouts  0.8 us

profile of v5, /device:TPU:6, one launch (start us, length us, event | category | flops | bytes accessed | tf_op | source)
XLA Modules:
  0.0 37.3 jit_solution(7809028057761902780)
XLA Ops:
  0.7 35.8 %shard_map.82 = bf16[1,256,1024]{2,1,0:T(8,128)(2,1)S(1)} custom-call(s32[1]{0:T(128)S(6)} %copy.10.slot_ref, bf16[1,2,64,4096]{3,2,1,0:T(8,128)(2,1)} %stash_ref.1, s32[1,2,64]{2,1,0:T(2,128)} %doc_hbm.1, bf16[4096]{0:T(1024)(128)(2,1)} %gain_hbm.1, f32[2,256,128]{2,1,0:T(8,128)} %constant.2.clone.table_hbm, bf16[4096,1024]{1,0:T(8,128)(2,1)} %wq_ref.1, ...), custom_call_target="tpu_custom_call" | custom-call | flops 3221225472 | bytes 12582912 | tf_op jit(solution)/shard_map/pallas_call | solution.py:706
  36.5 0.8 %copy.11 = bf16[1,256,1024]{2,1,0:T(8,128)(2,1)} copy(bf16[1,256,1024]{2,1,0:T(8,128)(2,1)S(1)} %shard_map.82) | data formatting | bytes 1048576

commit v6 on v5

--- a/solution.py
+++ b/solution.py
@@ -14,6 +14,8 @@
 NORM_EPSILON = 1e-05
 PIECES = 4
 HELD = 1
+SUBS = 32
+EDGES = (0, 9, 17, 24, 32)
 CHUNK = 16
 MESH = pl.DeviceIdType.MESH
 VMEM_GRANT = 32 << 20
@@ -54,9 +56,9 @@
     slots, rows, width = raw.shape
     pieces = PIECES
     part = width // pieces
-    half = part // 2
+    sub = width // SUBS
     nq, nk = wq_ref.shape[1], wk_ref.shape[1]
-    total_n = w.shape[2]
+    total_n = w.shape[1]
     total = n * rows
     hold = n > 2
     even, odd = sec % 2 == 0, sec % 2 == 1
@@ -86,11 +88,11 @@
         c.start()
 
     def w_copies():
-        for p in range(2 * pieces):
-            span = pl.ds(p * half, half)
-            yield pltpu.make_async_copy(wq_ref.at[span], w.at[p, :, 0:nq], w_sem)
-            yield pltpu.make_async_copy(wk_ref.at[span], w.at[p, :, nq:nq + nk], w_sem)
-            yield pltpu.make_async_copy(wv_ref.at[span], w.at[p, :, nq + nk:total_n], w_sem)
+        for p in range(pieces):
+            span = pl.ds(p * part, part)
+            yield pltpu.make_async_copy(wq_ref.at[span], w.at[span, 0:nq], w_sem)
+            yield pltpu.make_async_copy(wk_ref.at[span], w.at[span, nq:nq + nk], w_sem)
+            yield pltpu.make_async_copy(wv_ref.at[span], w.at[span, nq + nk:total_n], w_sem)
 
     gain_copy.wait()
     chosen = slot_ref[0]
@@ -108,8 +110,8 @@
         x = x.astype(jnp.float32)
         scale = lax.rsqrt(jnp.mean(x * x, axis=-1, keepdims=True) + NORM_EPSILON)
         y = (x * scale * gain_ref[...].astype(jnp.float32)[None, :]).astype(jnp.bfloat16)
-        for p in range(2 * pieces):
-            mine[p, r:r + CHUNK, :] = y[:, p * half:(p + 1) * half]
+        for p in range(SUBS):
+            mine[p, r:r + CHUNK, :] = y[:, p * sub:(p + 1) * sub]
     dmine[...] = jnp.zeros_like(dmine)
     doc_copy.wait()
     docs = doc_ref[0, 0:1, :]
@@ -134,21 +136,32 @@
             src_ref=src, dst_ref=dst, send_sem=ss, recv_sem=rs, device_id=target, device_id_type=MESH
         )
 
-    def sent(count, sem):
-        for m in range(1, pieces + 1):
-            @pl.when(count == m)
-            def _():
-                b = xbuf.at[0, pl.ds(0, 2 * m)]
-                remote(b, b, sem, sem, {"section": sec}).wait_send()
+    def sent(count, sem, amounts):
+        for m, amount in enumerate(amounts):
+            if amount:
+                @pl.when(count == m)
+                def _():
+                    b = xbuf.at[0, pl.ds(0, amount)]
+                    remote(b, b, sem, sem, {"section": sec}).wait_send()
+
+    def span_of(p):
+        return EDGES[p], EDGES[p + 1] - EDGES[p]
 
     def whole(p):
-        return pl.ds(2 * p, 2)
+        return pl.ds(*span_of(p))
+
+    low_half = (EDGES[-2], (SUBS - EDGES[-2]) // 2)
+    high_half = (EDGES[-2] + low_half[1], SUBS - EDGES[-2] - low_half[1])
 
     def first():
-        return pl.ds(2 * pieces - 2, 1)
+        return pl.ds(*low_half)
 
     def second():
-        return pl.ds(2 * pieces - 1, 1)
+        return pl.ds(*high_half)
+
+    def by_piece(p, body):
+        for q in range(pieces - 1):
+            pl.when(p == q)(functools.partial(body, q))
 
     def hop(src, c, p):
         return remote(src, xbuf.at[c, whole(p)], hop_send.at[c], recv.at[c, p], {"section": sec + 1})
@@ -195,9 +208,7 @@
             act(c)
 
     def pick(p, ordinary, last, act):
-        @pl.when(p < pieces - 1)
-        def _():
-            act(ordinary())
+        by_piece(p, lambda q: act(ordinary(q)))
 
         @pl.when(p == pieces - 1)
         def _():
@@ -277,13 +288,13 @@
 
     tile = 256
 
-    def compute(c, p, last, halves=2):
-        at = pl.ds(2 * p if halves == 2 else p, halves)
-        x = xbuf[c, at]
-        x = jnp.concatenate([x[j] for j in range(halves)], axis=1)
+    def compute(c, block, last):
+        here, size = block
+        x = xbuf[c, pl.ds(here, size)]
+        x = jnp.concatenate([x[j] for j in range(size)], axis=1)
+        deep = slice(here * sub, (here + size) * sub)
         for t in range(0, total_n, tile):
-            wt = w[at, :, t:t + tile].reshape(halves * half, tile)
-            acc[c, :, t:t + tile] += jnp.dot(x, wt, preferred_element_type=jnp.float32)
+            acc[c, :, t:t + tile] += jnp.dot(x, w[deep, t:t + tile], preferred_element_type=jnp.float32)
 
         if last is False:
             return
@@ -347,20 +358,21 @@
             attend(i)
 
     def own_forward(p):
-        held = (me == n - 2) & (p >= pieces - HELD) if hold else jnp.bool_(False)
-
+        held = (me == n - 2) if hold and p >= pieces - HELD else jnp.bool_(False)
+        last = p == pieces - 1
         both_ways(
             has_right & jnp.logical_not(held), has_left,
-            lambda: pick(p, lambda: right(me, p), lambda: right_last(me), start),
-            lambda: pick(p, lambda: left(me, p, True), lambda: left_last(me, True), start),
+            lambda: each(right_last(me) if last else [right(me, p)], start),
+            lambda: each(left_last(me, True) if last else [left(me, p, True)], start),
         )
 
     def compute_own(p):
-        @pl.when(p < early_prev)
-        def _():
-            shift(p).wait_recv()
-
-        compute(me, p, p == pieces - 1)
+        if p < pieces - 1:
+            @pl.when(p < early_prev)
+            def _():
+                shift(p).wait_recv()
+
+        compute(me, span_of(p), p == pieces - 1)
 
     def weights_here():
         table_copy.wait()
@@ -399,11 +411,8 @@
 
     def pass_all(d):
         if n > 1:
-            @pl.loop(0, pieces - 1)
-            def _(e):
-                @pl.when(e < early)
-                def _():
-                    pass_early(d, e)
+            for e in range(pieces - 1):
+                pl.when(e < early)(functools.partial(pass_early, d, e))
 
     @pl.when(has_prev)
     def _():
@@ -424,32 +433,32 @@
 
         keep_docs(me)
 
-        @pl.loop(early_prev, pieces)
-        def _(p):
-            pick(p, lambda: shift(p), shift_last, wait_recv)
+        def own_piece(p):
+            each(shift_last() if p == pieces - 1 else [shift(p)], wait_recv)
             own_forward(p)
 
-            @pl.when(p == jnp.where(even, early_prev, pieces - 1))
+            @pl.when((p == early_prev) & even | (p == pieces - 1) & odd)
             def _():
                 pass_all(1)
 
+        for p in range(pieces):
+            pl.when(p >= early_prev)(functools.partial(own_piece, p))
+
         @pl.when(at_end)
         def _():
             weights_here()
 
-            @pl.loop(0, pieces)
-            def _(p):
+            for p in range(pieces):
                 compute_own(p)
 
         attend_range(0, jnp.where((me == 0) & (n > 1), 1, 0))
 
     def take_early(c):
-        @pl.loop(0, pieces - 1)
-        def _(p):
+        for p in range(pieces - 1):
             @pl.when(p < early_prev)
             def _():
                 hop(xbuf.at[c, whole(p)], c, p).wait_recv()
-                compute(c, p, False)
+                compute(c, span_of(p), False)
 
     def drain():
         @pl.when(has_prev)
@@ -466,7 +475,7 @@
             @pl.when(has_left)
             def _():
                 dleft(me, True).wait_send()
-                sent(pieces - early_prev, left_send)
+                sent(early_prev, left_send, [SUBS - e for e in EDGES[:-1]])
 
             for d in range(1, n):
                 below, above = me - d, me + d
@@ -492,13 +501,13 @@
         @pl.when(has_next)
         def _():
             dshift().wait_send()
-            sent(pieces, hop_send.at[me])
+            sent(0, hop_send.at[me], [SUBS])
 
             @pl.when(early > 0)
             def _():
                 @pl.when(has_left)
                 def _():
-                    sent(early, zleft_send)
+                    sent(early, zleft_send, EDGES[:-1])
 
                 @pl.when(has_right)
                 def _():
@@ -512,7 +521,7 @@
 
                     @pl.when(below >= 0)
                     def _():
-                        sent(early, hop_send.at[below])
+                        sent(early, hop_send.at[below], EDGES[:-1])
 
                         @pl.when(has_right)
                         def _():
@@ -523,7 +532,7 @@
 
                     @pl.when(above < n)
                     def _():
-                        sent(early, hop_send.at[above])
+                        sent(early, hop_send.at[above], EDGES[:-1])
 
                         @pl.when(has_left)
                         def _():
@@ -535,7 +544,7 @@
     def take_last(c):
         for t, r in enumerate(right_last(c)):
             r.wait_recv()
-            compute(c, 2 * pieces - 2 + t, t == 1, 1)
+            compute(c, (low_half, high_half)[t], t == 1)
 
     def pass_now(d, p):
         @pl.when(jnp.where(even, (p == pieces - 1) & (d < n - 1), (p == 0) & (d > 1)))
@@ -571,7 +580,7 @@
 
             @pl.when(late & (below >= 0))
             def _():
-                pick(p, lambda: right(below, p), lambda: right_last(below), forward)
+                pick(p, lambda q: right(below, q), lambda: right_last(below), forward)
 
             if hold:
                 @pl.when((me == n - 2) & (d == n - 2) & final)
@@ -584,7 +593,7 @@
 
             @pl.when(late & (above < n))
             def _():
-                pick(p, lambda: left(above, p), lambda: left_last(above), forward)
+                pick(p, lambda q: left(above, q), lambda: left_last(above), forward)
 
             @pl.when(i == 0)
             def _():
@@ -592,25 +601,32 @@
 
             @pl.when((p == pieces - 2) & (early_prev > 0))
             def _():
-                @pl.when(below >= 0)
-                def _():
-                    take_early(below)
-
-                @pl.when(above < n)
-                def _():
-                    take_early(above)
-
-            @pl.when(d == min(2, n - 1))
-            def _():
-                compute_own(p)
-
-            @pl.when(late & (below >= 0))
-            def _():
-                compute(below, p, final)
-
-            @pl.when(late & (above < n))
-            def _():
-                compute(above, p, final)
+                @pl.loop(0, 2)
+                def _(j):
+                    c = jnp.where(j == 0, below, above)
+
+                    @pl.when((c >= 0) & (c < n))
+                    def _():
+                        take_early(c)
+
+            def middle_piece(q):
+                @pl.loop(0, 3)
+                def _(j):
+                    c = jnp.where(j == 0, me, jnp.where(j == 1, below, above))
+                    inside = (c >= 0) & (c < n)
+                    own = (j == 0) & (d == min(2, n - 1))
+
+                    if q < pieces - 1:
+                        @pl.when(own & (q < early_prev))
+                        def _():
+                            shift(q).wait_recv()
+
+                    @pl.when(own | (j > 0) & late & inside)
+                    def _():
+                        compute(c, span_of(q), q == pieces - 1)
+
+            for q in range(pieces):
+                pl.when(p == q)(functools.partial(middle_piece, q))
 
         attend_range(0, n)
 
@@ -653,12 +669,15 @@
             def _():
                 take_early(jnp.where(sooner, jnp.where(me == 0, n - 1, 0), c))
 
-            @pl.when(go & (p < pieces - 1))
-            def _():
-                right(c, p).wait_recv()
-                compute(c, p, False)
-
-            @pl.when(go & (p == pieces - 1) & (i < (n - 1) * pieces - 1))
+            def end_piece(q):
+                right(c, q).wait_recv()
+                compute(c, span_of(q), False)
+
+            @pl.when(go)
+            def _():
+                by_piece(p, end_piece)
+
+            @pl.when(go & (p == pieces - 1) & ((i < (n - 1) * pieces - 1) | (me > 0)))
             def _():
                 take_last(c)
 
@@ -668,14 +687,13 @@
 
         @pl.when(me > 0)
         def _():
-            take_last(0)
             if hold:
                 attend_range(0, n - 2)
                 for p in range(pieces - HELD, pieces - 1):
                     @pl.when(p >= early_prev)
                     def _():
                         right(n - 2, p).wait_recv()
-                        compute(n - 2, p, False)
+                        compute(n - 2, span_of(p), False)
 
                 take_last(n - 2)
             for t in range(max(n - 2, 0), n):
@@ -700,7 +718,6 @@
     table = rope_tables(total)
     lanes = -(-rows // 128) * 128
     bf, f32, dma = jnp.bfloat16, jnp.float32, pltpu.SemaphoreType.DMA
-    part = width // PIECES
     heads, stacked = nk // HEAD_SIZE, nq // nk * rows
     operands = (stash, doc_ids, norm_gain, jnp.asarray(table), w_query, w_key, value_weight)
     return pl.pallas_call(
@@ -710,11 +727,11 @@
         out_specs=VMEM,
         scratch_shapes=[
             pltpu.VMEM((slots, rows, width), bf),
-            pltpu.VMEM((2 * PIECES, rows, part // 2), bf),
+            pltpu.VMEM((SUBS, rows, width // SUBS), bf),
             pltpu.VMEM((8, lanes), jnp.int32),
-            pltpu.VMEM((2 * PIECES, part // 2, total_n), bf),
-            pltpu.VMEM((n, 2 * PIECES, rows, part // 2), bf),
-            pltpu.VMEM((n, 2 * PIECES - 2, rows, part // 2), bf),
+            pltpu.VMEM((width, total_n), bf),
+            pltpu.VMEM((n, SUBS, rows, width // SUBS), bf),
+            pltpu.VMEM((n, EDGES[-2], rows, width // SUBS), bf),
             pltpu.VMEM((n, 8, lanes), jnp.int32),
             pltpu.VMEM((n, rows, total_n), f32),
             pltpu.VMEM((total, nq), bf),

time: 37.5 us -> 37.2 us (level)
  Pallas kernels: 35.8 us -> 35.3 us
    pallas_call x1, Pallas kernels: 35.8 us -> 35.3 us  [per_device(): pl.pallas_call(functools.partial(kernel, n, ns), out_shape=jax.ShapeDtype...]
where the time goes in v6:
time: 37.2 us; the launch traced here: 36.8 us
  Pallas kernels  35.3 us (95%)
  local copies, waits for them, and re-layouts  0.8 us (2%)
  between operations  0.66 us (2%)
    pallas_call x1, Pallas kernels, per_device(): pl.pallas_call(functools.partial(kernel, n, ns), out_shape=jax.ShapeDtype...  35.3 us
    unnamed x1, local copies, waits for them, and re-layouts  0.8 us

profile of v6, /device:TPU:6, one launch (start us, length us, event | category | flops | bytes accessed | tf_op | source)
XLA Modules:
  0.0 36.8 jit_solution(17382445181326526627)
XLA Ops:
  0.7 35.3 %shard_map.82 = bf16[1,256,1024]{2,1,0:T(8,128)(2,1)S(1)} custom-call(s32[1]{0:T(128)S(6)} %copy.10.slot_ref, bf16[1,2,64,4096]{3,2,1,0:T(8,128)(2,1)} %stash_ref.1, s32[1,2,64]{2,1,0:T(2,128)} %doc_hbm.1, bf16[4096]{0:T(1024)(128)(2,1)} %gain_hbm.1, f32[2,256,128]{2,1,0:T(8,128)} %constant.2.clone.table_hbm, bf16[4096,1024]{1,0:T(8,128)(2,1)} %wq_ref.1, ...), custom_call_target="tpu_custom_call" | custom-call | flops 3221225472 | bytes 12582912 | tf_op jit(solution)/shard_map/pallas_call | solution.py:723
  36.0 0.8 %copy.11 = bf16[1,256,1024]{2,1,0:T(8,128)(2,1)} copy(bf16[1,256,1024]{2,1,0:T(8,128)(2,1)S(1)} %shard_map.82) | data formatting | bytes 1048576

commit v7 on v6

--- a/solution.py
+++ b/solution.py
@@ -98,12 +98,6 @@
     chosen = slot_ref[0]
     pltpu.make_async_copy(raw, raw, hop_send.at[0]).wait()
     for i, r in enumerate(starts):
-        if i == 0:
-            @pl.when(has_prev)
-            def _():
-                table_copy.start()
-                for c in w_copies():
-                    c.start()
         x = raw[0, r:r + CHUNK, :]
         for j in range(1, slots):
             x = jnp.where(jnp.full(x.shape, chosen, jnp.int32) == j, raw[j, r:r + CHUNK, :], x)
@@ -285,6 +279,12 @@
         def _():
             hops()
             own_ways()
+
+    @pl.when(has_prev)
+    def _():
+        table_copy.start()
+        for c in w_copies():
+            c.start()
 
     tile = 256
 

time: 37.2 us -> 37.2 us (level)
  no operation moved by 1% of the time
where the time goes in v7:
time: 37.2 us; the launch traced here: 36.8 us
  Pallas kernels  35.3 us (95%)
  local copies, waits for them, and re-layouts  0.8 us (2%)
  between operations  0.66 us (2%)
    pallas_call x1, Pallas kernels, per_device(): pl.pallas_call(functools.partial(kernel, n, ns), out_shape=jax.ShapeDtype...  35.3 us
    unnamed x1, local copies, waits for them, and re-layouts  0.8 us

profile of v7, /device:TPU:6, one launch (start us, length us, event | category | flops | bytes accessed | tf_op | source)
XLA Modules:
  0.0 36.8 jit_solution(10222351509081087440)
XLA Ops:
  0.7 35.3 %shard_map.82 = bf16[1,256,1024]{2,1,0:T(8,128)(2,1)S(1)} custom-call(s32[1]{0:T(128)S(6)} %copy.10.slot_ref, bf16[1,2,64,4096]{3,2,1,0:T(8,128)(2,1)} %stash_ref.1, s32[1,2,64]{2,1,0:T(2,128)} %doc_hbm.1, bf16[4096]{0:T(1024)(128)(2,1)} %gain_hbm.1, f32[2,256,128]{2,1,0:T(8,128)} %constant.2.clone.table_hbm, bf16[4096,1024]{1,0:T(8,128)(2,1)} %wq_ref.1, ...), custom_call_target="tpu_custom_call" | custom-call | flops 3221225472 | bytes 12582912 | tf_op jit(solution)/shard_map/pallas_call | solution.py:723
  36.0 0.8 %copy.11 = bf16[1,256,1024]{2,1,0:T(8,128)(2,1)} copy(bf16[1,256,1024]{2,1,0:T(8,128)(2,1)S(1)} %shard_map.82) | data formatting | bytes 1048576
